TPU v7x, 512 devices: a 8x2x16 block of a 8x8x16 slice. The times are simulated.
512 devices in a mesh: ga: 2 (over y), gx: 16 (over z), gy: 8 (over x), col: 2 (over core).
Axes of the slice: x: 8, y: 2, z: 16, core: 2. Of those that a mesh axis runs over, the one named last changes fastest.
The devices are a block of a 8x8x16 slice.
Arguments:
- pair_rep: bfloat16 [2, 640, 640, 128], P('ga', 'gx', 'gy'), parts along dimension 0, may hold values from -6 to 6
- pair_mask: int32 [2, 640, 640], P('ga', 'gx', 'gy'), parts along dimension 0, may hold values 0 or 1
- amax_history: float32 [2, 128], P(None, 'col'), may hold values from 0.3 to 3
- in_gain: float32 [128], replicated, may hold values from 0.5 to 1.5
- in_bias: float32 [128], replicated, may hold values from -3 to 3
- proj_weight: bfloat16 [128, 4, 128], P(None, None, 'col'), may hold values from -0.5 to 0.5
- gate_weight: bfloat16 [128, 128], P(None, 'col'), may hold values from -0.5 to 0.5
- out_gain: float32 [128], replicated, may hold values from 0.5 to 1.5
- out_bias: float32 [128], replicated, may hold values from -3 to 3
- out_weight: bfloat16 [128, 128], P(None, 'col'), may hold values from -0.5 to 0.5
Outputs:
- update: bfloat16 [2, 640, 640, 128], P('ga', 'gx', 'gy', 'col'), parts along dimension 0
- new_amax: float32 [4, 128], P('ga', 'col'), parts along dimension 0
There are 2 independent parts, one for each index of `ga`. A program takes and returns all parts, laid end to end along the dimension named above; an argument that names none is the same for every part. Nothing has to cross between parts.
All inputs are finite; a program needn't handle non-finite values. No bound on the sum of `pair_mask` on one device may be relied on, other than what follows from the above.
Results may differ from a plain program's by a relative error of at most 0.0065.
Values may be sent and summed in bfloat16 or wider, within the bound.
No kernel may reach another device: no remote copies, remote signals or barrier semaphores. Data moves between devices by JAX's collectives and lax.ppermute only.
A program may use at most 128 MiB of HBM per device.

v0:
```python
import jax
import jax.numpy as jnp
from jax import lax
from jax.sharding import PartitionSpec as P

epsilon = 1e-05
format_limit = 448.0


def broadcast(block, axis, holder):
    block = jnp.where(lax.axis_index(axis) == holder, block, jnp.zeros_like(block))
    return lax.psum(block, axis)


def copy_for_each(array, axis):
    copies = jnp.broadcast_to(array, (lax.axis_size(axis), *array.shape))
    return lax.all_to_all(copies, axis, split_axis=0, concat_axis=0, tiled=True)


def joined_along(parts, dim):
    dims = list(parts.shape[1:])
    dims[dim] *= parts.shape[0]
    return jnp.moveaxis(parts, 0, dim).reshape(dims)


def gather_directly(array, axis, dim):
    parts = copy_for_each(array, axis)
    return joined_along(parts, dim)


def total_of_pieces(array, axis):
    parts = lax.all_gather(array, axis)
    return parts.max(axis=0)


def layer_norm(values, gain, bias):
    average = jnp.mean(values, axis=-1, keepdims=True)
    spread = jnp.mean(jnp.square(values - average), axis=-1, keepdims=True)
    return (values - average) * lax.rsqrt(spread + epsilon) * gain + bias


def crop_triangle(left_q, right_q):
    wide_rows = lax.all_gather(right_q, "gy", axis=2, tiled=True)
    row_ratio = lax.axis_size("gx") // lax.axis_size("gy")
    first_root = lax.axis_index("gy") * row_ratio
    received = [
        broadcast(wide_rows, "gx", first_root + offset_step) for offset_step in range(row_ratio)
    ]
    panel = jnp.concatenate(received, axis=1)
    return jnp.einsum(
        "cik,cjk->cij", gather_directly(left_q, "gy", 2), panel, preferred_element_type=jnp.float32
    )


def on_device(
    pair_rep,
    pair_mask,
    amax_history,
    in_gain,
    in_bias,
    proj_weight,
    gate_weight,
    out_gain,
    out_bias,
    out_weight,
):
    normed = layer_norm(pair_rep.astype(jnp.float32), in_gain, in_bias).astype(jnp.bfloat16)
    projected = jnp.einsum(
        "bikd,dsc->scbik", normed, proj_weight, preferred_element_type=jnp.float32
    )
    masking = pair_mask.astype(jnp.float32)[None]
    left_proj = masking * jax.nn.sigmoid(projected[1]) * projected[0]
    right_proj = masking * jax.nn.sigmoid(projected[3]) * projected[2]
    local_max = jnp.stack(
        [jnp.max(jnp.abs(left_proj), axis=(1, 2, 3)), jnp.max(jnp.abs(right_proj), axis=(1, 2, 3))]
    )
    new_amax = total_of_pieces(local_max, ("gx", "gy"))
    scales = amax_history / format_limit
    left_q = jnp.clip(
        left_proj / scales[0][:, None, None, None], -format_limit, format_limit
    ).astype(jnp.bfloat16)
    right_q = jnp.clip(
        right_proj / scales[1][:, None, None, None], -format_limit, format_limit
    ).astype(jnp.bfloat16)
    products = jnp.stack([crop_triangle(left_q[:, 0], right_q[:, 0])], axis=1)
    triangle = (products * (scales[0] * scales[1])[:, None, None, None]).astype(jnp.bfloat16)
    gathered = lax.all_gather(triangle, "col", axis=0, tiled=True).astype(jnp.float32)
    average = jnp.mean(gathered, axis=0, keepdims=True)
    spread = jnp.mean(jnp.square(gathered - average), axis=0, keepdims=True)
    tnorm = (
        (gathered - average) * lax.rsqrt(spread + epsilon) * out_gain[:, None, None, None]
        + out_bias[:, None, None, None]
    ).astype(jnp.bfloat16)
    mixing = jnp.einsum("cbij,cd->bijd", tnorm, out_weight, preferred_element_type=jnp.float32)
    gating = jax.nn.sigmoid(
        jnp.einsum("bijd,dc->bijc", normed, gate_weight, preferred_element_type=jnp.float32)
    )
    update = (gating * mixing).astype(jnp.bfloat16)
    return (update, new_amax)


def solution(mesh):
    placed = (
        P("ga", "gx", "gy", None),
        P("ga", "gx", "gy"),
        P(None, "col"),
        P(),
        P(),
        P(None, None, "col"),
        P(None, "col"),
        P(),
        P(),
        P(None, "col"),
    )
    return jax.shard_map(
        on_device,
        mesh=mesh,
        in_specs=placed,
        out_specs=(P("ga", "gx", "gy", "col"), P("ga", "col")),
        check_vma=False,
    )
```

profile of v0, /device:TPU:65, one launch (start us, length us, event | category | flops | bytes accessed | tf_op | source)
XLA Modules:
  0.0 403.0 jit_solution(6059494972928307105)
XLA Ops:
  7.3 0.7 broadcast_multiply_fusion.2
  8.0 0.7 convert_bitcast_fusion.1
  8.8 1.6 convert_reduce_fusion.1
  10.4 2.3 fusion.13
  12.8 2.1 convolution_bitcast_fusion
  14.9 2.3 fusion.45
  17.4 1.3 copy.23
  18.8 117.4 %all-gather.5.cloned.1.call-done = bf16[64,40,640]{0,1,2:T(8,128)(2,1)} async-done(((bf16[64,40,80]{0,1,2:T(8,128)(2,1)}), bf16[64,40,640]{0,1,2:T(8,128)(2,1)}) %all-gather.5.cloned.1.call-update) | async-done | bytes 3276816 | tf_op jit(solution)/shard_map/all_gather | solution.py:43
  136.3 14.6 %copy.24 = bf16[64,40,640]{2,1,0:T(8,128)(2,1)S(1)} copy(bf16[64,40,640]{0,1,2:T(8,128)(2,1)} %all-gather.5.cloned.1.call-done) | data formatting | bytes 6553600 | tf_op jit(solution)/shard_map/all_gather | solution.py:43
  150.8 3.3 broadcast_select_fusion.1
  154.2 1.0 copy-done.4
  155.6 3.0 broadcast_in_dim.2
  158.6 4.8 %all-to-all-start = ((bf16[8,64,40,80]{3,2,1,0:T(8,128)(2,1)}), bf16[8,64,40,80]{3,2,1,0:T(8,128)(2,1)}, u32[]{:S(2)}, u32[]{:S(2)}) async-start(bf16[8,64,40,80]{3,2,1,0:T(8,128)(2,1)} %broadcast_in_dim.2), calls=%async_computation | async-start | bytes 10485760 | tf_op jit(solution)/shard_map/all_to_all | solution.py:17
  163.5 3.5 fusion.37
  167.0 185.1 %all-gather.2 = f32[128,2,64]{2,1,0:T(2,128)S(1)} all-gather(f32[1,2,64]{2,1,0:T(2,128)S(1)} %maximum_bitcast_fusion), channel_id=3, replica_groups=mesh['ga'=2,'gx'=16,'gy'=8,'col'=2] {'gx','gy'}, dimensions={0}, use_global_device_ids=true | all-gather | bytes 66048 | tf_op jit(solution)/shard_map/all_gather | solution.py:32
  352.2 0.7 reduce_max.29
  352.9 2.3 fusion.19
  355.2 10.9 %copy.21 = bf16[64,40,8,80]{3,2,1,0:T(8,128)(2,1)} copy(bf16[64,40,8,80]{3,1,0,2:T(8,128)(2,1)} %bitcast.10) | data formatting | bytes 6553600 | tf_op jit(solution)/shard_map/transpose | solution.py:23
  366.1 7.2 %reshape.236 = bf16[64,40,640]{2,1,0:T(8,128)(2,1)S(1)} reshape(bf16[64,40,8,80]{3,2,1,0:T(8,128)(2,1)} %copy.21) | data formatting | bytes 6553600 | tf_op jit(solution)/shard_map/reshape | solution.py:23
  373.3 5.1 %fusion.23 = bf16[64,40,80]{2,1,0:T(8,128)(2,1)S(1)} fusion(bf16[64,40,640]{2,1,0:T(8,128)(2,1)S(1)} %reshape.236, bf16[64,40,640]{2,1,0:T(8,128)(2,1)} %get-tuple-element.4, bf16[64,40,640]{2,1,0:T(8,128)(2,1)} %get-tuple-element.5, f32[64]{0:T(128)S(1)} %fusion.58), kind=kOutput, calls=%fused_computation.30 | convolution fusion | flops 275660800 | bytes 10240256 | tf_op jit(solution)/shard_map/cik,cjk->cij/dot_general | solution.py:50
  378.4 14.5 %all-gather = bf16[128,40,80]{2,1,0:T(8,128)(2,1)S(1)} all-gather(bf16[64,40,80]{2,1,0:T(8,128)(2,1)S(1)} %fusion.23), channel_id=2, replica_groups=mesh['ga'=2,'gx'=16,'gy'=8,'col'=2] {'col'}, dimensions={0}, use_global_device_ids=true | all-gather | bytes 1228800 | tf_op jit(solution)/shard_map/all_gather | solution.py:87
  393.7 0.5 fusion.27
  394.3 0.7 copy-done.5
  395.0 1.2 fusion.47
  (38 shorter events, 1.8 us)
Async XLA Ops:
  7.2 5.5 %copy-start = (bf16[128,4,64]{0,2,1:T(8,128)(2,1)S(1)}, bf16[128,4,64]{0,2,1:T(8,128)(2,1)}, u32[]{:S(2)}) copy-start(bf16[128,4,64]{0,2,1:T(8,128)(2,1)} %param.15) | copy-start | bytes 196612
  7.2 5.5 %copy-start.2 = (bf16[1,40,80,128]{3,2,1,0:T(8,128)(2,1)S(1)}, bf16[1,40,80,128]{3,2,1,0:T(8,128)(2,1)}, u32[]{:S(2)}) copy-start(bf16[1,40,80,128]{3,2,1,0:T(8,128)(2,1)} %param.10) | copy-start | bytes 2457604
  7.2 5.5 %copy-start.7 = (f32[128]{0:T(128)S(1)}, f32[128]{0:T(128)}, u32[]{:S(2)}) copy-start(f32[128]{0:T(128)} %param.14) | copy-start | bytes 1540
  7.2 5.5 %copy-start.8 = (f32[128]{0:T(128)S(1)}, f32[128]{0:T(128)}, u32[]{:S(2)}) copy-start(f32[128]{0:T(128)} %param.13) | copy-start | bytes 1540
  7.2 129.0 %all-gather.5.cloned.1.call-start = ((), (), s32[]{:S(2)}) async-start(), calls=%async_computation.1 | async-start | bytes 7372800 | tf_op jit(solution)/shard_map/all_gather | solution.py:43
  14.9 2.5 copy-start.1
  18.8 354.5 %all-reduce.3.cloned.1.call-start = ((), (), s32[]{:S(2)}) async-start(), calls=%async_computation.2 | async-start | bytes 13107200 | tf_op jit(solution)/shard_map/psum | solution.py:12
  154.1 1.1 copy-start.4
  158.6 196.6 %all-to-all-start = ((bf16[8,64,40,80]{3,2,1,0:T(8,128)(2,1)}), bf16[8,64,40,80]{3,2,1,0:T(8,128)(2,1)}, u32[]{:S(2)}, u32[]{:S(2)}) async-start(bf16[8,64,40,80]{3,2,1,0:T(8,128)(2,1)} %broadcast_in_dim.2), calls=%async_computation | async-start | bytes 10485760 | tf_op jit(solution)/shard_map/all_to_all | solution.py:17
  163.5 189.4 %copy-start.3 = (bf16[1,40,80,128]{3,2,1,0:T(8,128)(2,1)S(1)}, bf16[1,40,80,128]{3,2,1,0:T(8,128)(2,1)}, u32[]{:S(2)}) copy-start(bf16[1,40,80,128]{3,2,1,0:T(8,128)(2,1)} %param.10) | copy-start | bytes 2457604
  163.5 189.4 %copy-start.11 = (bf16[128,64]{0,1:T(8,128)(2,1)S(1)}, bf16[128,64]{0,1:T(8,128)(2,1)}, u32[]{:S(2)}) copy-start(bf16[128,64]{0,1:T(8,128)(2,1)} %param.16) | copy-start | bytes 49156
  392.9 0.8 copy-start.9
  392.9 0.8 copy-start.10
  393.7 1.3 copy-start.5
  393.7 1.3 copy-start.6
Sparse Core Ops, SparseCore 0:
  18.9 117.3 all-gather.4
  154.3 179.9 all-reduce.2
where the time goes:
time: 404 us; the launch traced here: 403 us
  blocking collectives  200 us (50%)
  waiting for transfers between devices  118 us (29%)
  local copies, waits for them, and re-layouts  39.4 us (10%)
  other arithmetic  16.5 us (4%)
  between operations  14.3 us (4%)
  matrix products  10.7 us (3%)
  starting transfers between devices  4.97 us (1%)
    all_gather x1, blocking collectives, total_of_pieces(): parts = lax.all_gather(array, axis)  185 us
    all_gather x1, waiting for transfers between devices, crop_triangle(): wide_rows = lax.all_gather(right_q, 'gy', axis=2, tiled=True)  117 us
    all_gather x1, local copies, waits for them, and re-layouts, crop_triangle(): wide_rows = lax.all_gather(right_q, 'gy', axis=2, tiled=True)  14.6 us
    all_gather x1, blocking collectives, on_device(): lax.all_gather(triangle, 'col', axis=0, tiled=True).astype(jnp.float32)  14.5 us
    transpose x1, local copies, waits for them, and re-layouts, joined_along(): return jnp.moveaxis(parts, 0, dim).reshape(dims)  10.9 us
  transfers between devices with their start and end apart: 3, of which 1 were waited for; matrix products, arithmetic and copies ran while one was open for 7% of the time, Pallas kernels for 0%

commit v1 on v0

v1 whole, which is shorter than its diff:
```python
import functools

import jax
import jax.numpy as jnp
from jax import lax
from jax.experimental import pallas as pl
from jax.experimental.pallas import tpu as pltpu
from jax.sharding import PartitionSpec as P

epsilon = 1e-05
format_limit = 448.0
LANES = 128
F32 = jnp.float32
BF16 = jnp.bfloat16


def lane_round(size):
    return -(-size // LANES) * LANES


def normed_rows(rows, gain, bias):
    average = jnp.mean(rows, axis=-1, keepdims=True)
    spread = jnp.mean(jnp.square(rows - average), axis=-1, keepdims=True)
    return ((rows - average) * lax.rsqrt(spread + epsilon) * gain + bias).astype(BF16)


def one_hot_rows(channels, parity, dtype=BF16):
    row = lax.broadcasted_iota(jnp.int32, (2 * channels, channels), 0)
    col = lax.broadcasted_iota(jnp.int32, (2 * channels, channels), 1)
    return jnp.where(row == 2 * col + parity, 1.0, 0.0).astype(dtype)


def one_hot_cols(channels, parity):
    row = lax.broadcasted_iota(jnp.int32, (channels, 2 * channels), 0)
    col = lax.broadcasted_iota(jnp.int32, (channels, 2 * channels), 1)
    return jnp.where(col == 2 * row + parity, 1.0, 0.0).astype(BF16)


def nn(left, right):
    return jnp.dot(left, right, preferred_element_type=F32)


def nt(left, right):
    return lax.dot_general(left, right, (((1,), (1,)), ((), ())), preferred_element_type=F32)


def split_parts(values):
    high = values.astype(BF16).astype(F32)
    middle = (values - high).astype(BF16).astype(F32)
    return high, middle, values - high - middle


def project_kernel(
    half_ref, rep_ref, mask_ref, weight_ref, inverse_ref, gain_ref, bias_ref, out_ref, near, far, proj
):
    rows, cols, channels = rep_ref.shape
    deep = rows // 4
    span = deep * cols
    wide = near.shape[0]
    shift = span - (wide - LANES)
    half = half_ref[0]
    gain, bias = gain_ref[...], bias_ref[...]
    near[pl.ds(span, wide - span), :] = jnp.zeros((wide - span, 2 * channels), BF16)
    far[pl.ds(0, shift), :] = jnp.zeros((shift, 2 * channels), BF16)
    far[pl.ds(shift + span, wide - span - shift), :] = jnp.zeros((wide - span - shift, 2 * channels), BF16)
    for part in range(2):
        for at in range(deep):
            block = rep_ref[half * (2 * deep) + part * deep + at].astype(F32)
            block = normed_rows(block, gain, bias)
            near[at * cols : (at + 1) * cols, part * channels : (part + 1) * channels] = block
            far[shift + at * cols : shift + (at + 1) * cols, part * channels : (part + 1) * channels] = block
    even, odd = one_hot_rows(channels, 0), one_hot_rows(channels, 1)
    for which in range(4):
        weight = jnp.concatenate([weight_ref[0, which], weight_ref[1, which]], axis=0)
        weight = jnp.concatenate([nn(even, weight), nn(odd, weight)], axis=1).astype(BF16)
        proj[which] = nt(weight, (near if which < 2 else far)[...])
    masks = mask_ref[...].astype(F32)
    masks = jnp.where(half == 0, masks[: 2 * deep], masks[2 * deep :])
    pieces = [
        jnp.concatenate([masks[at : at + 1], masks[deep + at : deep + at + 1]], axis=0)
        for at in range(deep)
    ]
    zeros = jnp.zeros((2, wide - span), F32)
    mask_near = jnp.concatenate([*pieces, zeros], axis=1)
    mask_far = pltpu.roll(jnp.concatenate([mask_near] * 4, axis=0), shift, 1)
    mask_near = jnp.concatenate([mask_near] * 8, axis=0)
    mask_far = jnp.concatenate([mask_far] * 2, axis=0)
    lane = lax.broadcasted_iota(jnp.int32, (16, LANES), 1)
    first = shift + span - (wide - LANES)

    def step(at, carry):
        rows_at = pl.ds(pl.multiple_of(at * 16, 16), 16)
        left = mask_near * jax.nn.sigmoid(proj[1, rows_at, :]) * proj[0, rows_at, :]
        right = mask_far * jax.nn.sigmoid(proj[3, rows_at, :]) * proj[2, rows_at, :]
        left_max = jnp.max(jnp.abs(left), axis=1, keepdims=True)
        right_max = jnp.max(jnp.abs(right), axis=1, keepdims=True)
        inverse = inverse_ref[rows_at, :]
        left = jnp.clip(left * inverse[:, 0:1], -format_limit, format_limit)
        right = jnp.clip(right * inverse[:, 1:2], -format_limit, format_limit)
        edge = wide - LANES
        out_ref[rows_at, 0:edge] = left[:, :edge].astype(BF16)
        out_ref[rows_at, edge:wide] = (left[:, edge:] + right[:, :LANES]).astype(BF16)
        out_ref[rows_at, wide : wide + edge - LANES] = right[:, LANES:edge].astype(BF16)
        last = right[:, edge:]
        for place, part in enumerate((*split_parts(left_max), *split_parts(right_max))):
            last = jnp.where(lane == first + place, part, last)
        out_ref[rows_at, wide + edge - LANES : wide + edge] = last.astype(BF16)
        return carry

    lax.fori_loop(0, 2 * channels // 16, step, 0)


def gate_kernel(
    rep_ref, gate_ref, weight_ref, gain_ref, bias_ref, gating_ref, mixer_ref, order_ref, near
):
    rows, cols, channels = rep_ref.shape
    deep = rows // 4
    span = deep * cols
    outs = gate_ref.shape[0]
    gain, bias = gain_ref[...], bias_ref[...]
    blank = jnp.zeros((outs, channels), BF16)
    gate = gate_ref[...]
    wide_gate = jnp.concatenate(
        [jnp.concatenate([gate, blank], axis=1), jnp.concatenate([blank, gate], axis=1)], axis=0
    )
    near[span:, :] = jnp.zeros((near.shape[0] - span, 2 * channels), BF16)
    for half in range(2):
        for part in range(2):
            for at in range(deep):
                block = rep_ref[half * (2 * deep) + part * deep + at].astype(F32)
                near[at * cols : (at + 1) * cols, part * channels : (part + 1) * channels] = normed_rows(
                    block, gain, bias
                )
        gating_ref[half] = jax.nn.sigmoid(nt(wide_gate, near[...]))
    weight = weight_ref[...]
    mixer_ref[0:outs, :] = nn(weight, one_hot_cols(channels, 0)).astype(BF16)
    mixer_ref[outs:, :] = nn(weight, one_hot_cols(channels, 1)).astype(BF16)
    count, lanes = order_ref.shape
    per_half = count // 2
    per_at = per_half // deep
    pairs = cols // rows
    step = 32
    for start in range(0, count, step):
        row = start + lax.broadcasted_iota(jnp.int32, (step, 1), 0)
        half_at = start // per_half
        deep_at = (start % per_half) // per_at
        block = (row - half_at * per_half - deep_at * per_at) >> 1
        part = row & 1
        target = (block // pairs) * LANES + (block % pairs) * rows + half_at * 2 * deep + part * deep + deep_at
        lane = lax.broadcasted_iota(jnp.int32, (step, lanes), 1)
        order_ref[start : start + step, :] = jnp.where(lane == target, 1.0, 0.0).astype(BF16)


def triangle_kernel(
    scale_ref, own_ref, both_ref, order_ref, out_ref, left, right, moved, *, groups, deep, cols
):
    rows, wide = both_ref.shape[1:]
    block = rows // groups
    span = deep * cols
    first = span - (wide - LANES)
    used = lax.broadcasted_iota(jnp.int32, (block, LANES), 1) < cols
    none = jnp.zeros((block, LANES), BF16)

    def window(ref, group, start):
        base = start // LANES * LANES
        rows_at = pl.ds(group * block, block)
        if start == base:
            return ref[rows_at, base : base + LANES]
        return ref[rows_at, base : base + 2 * LANES][:, start - base : start - base + LANES]

    for group in range(groups):
        for at in range(deep):
            piece = window(own_ref, group, at * cols)
            left[at * block : (at + 1) * block, group * LANES : (group + 1) * LANES] = jnp.where(used, piece, none)
            for other in range(2):
                place = (other * deep + at) * block
                right[place : place + block, group * LANES : (group + 1) * LANES] = window(
                    both_ref.at[other], group, first + at * cols
                )
    products = nt(left[...], right[...]) * scale_ref[0]
    moved[...] = nn(products.astype(BF16), order_ref[...]).astype(BF16)
    lane = lax.broadcasted_iota(jnp.int32, (8, LANES), 1)
    first = first + span - (wide - LANES)
    best = None
    for other in range(2):
        parts = both_ref[other, :, wide - LANES :].astype(F32)
        total = parts + pltpu.roll(parts, LANES - 1, 1) + pltpu.roll(parts, LANES - 2, 1)
        total = jnp.max(total.reshape(rows // 8, 8, LANES), axis=0)
        best = total if best is None else jnp.maximum(best, total)
    best = jnp.broadcast_to(jnp.max(best, axis=0, keepdims=True), (8, LANES))
    goal = span % LANES
    tail = jnp.zeros((8, LANES), F32)
    for place, part in enumerate(split_parts(best)):
        turned = pltpu.roll(part, (goal + place - first) % LANES, 1)
        tail = jnp.where((lane == goal + place) | (lane == goal + place + 3), turned, tail)
    tail = tail[0:1, goal:].astype(BF16)
    tail = jnp.broadcast_to(tail.astype(F32), (block, LANES - goal)).astype(BF16)
    for group in range(groups):
        pieces = [
            moved[at * block : (at + 1) * block, group * LANES : group * LANES + cols] for at in range(deep)
        ]
        out_ref[group * block : (group + 1) * block, :] = jnp.concatenate([*pieces, tail], axis=1)


def finish_kernel(
    half_ref, both_ref, gating_ref, mixer_ref, gain_ref, bias_ref, update_ref, amax_ref, mixed, *, deep, cols
):
    rows, wide = both_ref.shape[1:]
    channels = rows // 2
    outs = update_ref.shape[1]
    span = deep * cols
    gain, bias = gain_ref[...], bias_ref[...]
    mixer = mixer_ref[...]

    def per_part(values):
        total = jnp.sum(values, axis=0)
        total = total + pltpu.roll(total, 4, 0)
        total = total + pltpu.roll(total, 2, 0)
        return total * (1.0 / channels)

    for half in range(2):
        for start in range(0, wide, LANES):
            values = both_ref[half, :, start : start + LANES].astype(F32).reshape(rows // 8, 8, LANES)
            values = values - per_part(values)[None]
            spread = per_part(jnp.square(values))
            values = (values * lax.rsqrt(spread + epsilon)[None]).reshape(rows, LANES)
            tnorm = (values * gain + bias).astype(BF16)
            mixing = nn(mixer, tnorm)
            mixed[:, start : start + LANES] = (gating_ref[half, :, start : start + LANES] * mixing).astype(BF16)
        for part in range(2):
            for at in range(deep):
                place = half * 2 * deep + part * deep + at
                update_ref[place] = mixed[part * outs : (part + 1) * outs, at * cols : (at + 1) * cols]
    last = both_ref[0, :, wide - LANES :]
    row = lax.broadcasted_iota(jnp.int32, (rows, outs), 0)
    col = lax.broadcasted_iota(jnp.int32, (rows, outs), 1)
    chosen = jnp.where(row == 2 * (col + half_ref[0] * outs), 1.0, 0.0).astype(BF16)
    sums = lax.dot_general(last, chosen, (((0,), (0,)), ((), ())), preferred_element_type=F32)
    goal = span % LANES
    amax_ref[0:1, :] = sums[goal : goal + 1] + sums[goal + 1 : goal + 2] + sums[goal + 2 : goal + 3]
    amax_ref[1:2, :] = sums[goal + 3 : goal + 4] + sums[goal + 4 : goal + 5] + sums[goal + 5 : goal + 6]


VMEM = pl.BlockSpec(memory_space=pltpu.VMEM)
SMEM = pl.BlockSpec(memory_space=pltpu.SMEM)


def on_device(
    pair_rep,
    pair_mask,
    amax_history,
    in_gain,
    in_bias,
    proj_weight,
    gate_weight,
    out_gain,
    out_bias,
    out_weight,
):
    rows, cols, channels = pair_rep.shape[1:]
    deep = rows // 4
    span = deep * cols
    wide = lane_round(span)
    groups, ranks = lax.axis_size("gy"), lax.axis_size("gx")
    chips = ("gy", "gx")
    assert groups * ranks == channels and lax.axis_size("col") == 2
    half = lax.axis_index("col").reshape(1).astype(jnp.int32)
    rep = pair_rep[0]
    gain, bias = in_gain[None, :], in_bias[None, :]

    weights = lax.all_gather(jnp.transpose(proj_weight, (1, 2, 0)), "col")
    history = jnp.transpose(lax.all_gather(amax_history, "col"), (1, 0, 2)).reshape(2, channels)
    scales = history / format_limit
    inverse = jnp.repeat((1.0 / scales).T, 2, axis=0)
    message = pl.pallas_call(
        project_kernel,
        name="project",
        out_shape=jax.ShapeDtypeStruct((2 * channels, 2 * wide - LANES), BF16),
        in_specs=[SMEM] + [VMEM] * 6,
        out_specs=VMEM,
        scratch_shapes=[
            pltpu.VMEM((wide, 2 * channels), BF16),
            pltpu.VMEM((wide, 2 * channels), BF16),
            pltpu.VMEM((4, 2 * channels, wide), F32),
        ],
    )(half, rep, pair_mask[0], weights, inverse, gain, bias)
    received = lax.all_to_all(
        message.reshape(channels, 2, -1), chips, split_axis=0, concat_axis=0, tiled=True
    )
    gating, mixer, order = pl.pallas_call(
        gate_kernel,
        name="gate",
        out_shape=(
            jax.ShapeDtypeStruct((2, channels, wide), F32),
            jax.ShapeDtypeStruct((channels, 2 * channels), BF16),
            jax.ShapeDtypeStruct((ranks * rows, groups * LANES), BF16),
        ),
        in_specs=[VMEM] * 5,
        out_specs=(VMEM,) * 3,
        scratch_shapes=[pltpu.VMEM((wide, 2 * channels), BF16)],
        cost_estimate=pl.CostEstimate(flops=20_000_000_000, bytes_accessed=3_000_000, transcendentals=0),
    )(rep, gate_weight.T, out_weight.T, gain, bias)
    received = received.reshape(2 * channels, -1)
    edge = wide - LANES
    both = lax.all_gather(received[:, edge:], "col")
    mine = lax.axis_index(chips)
    scale = lax.dynamic_slice(scales[0] * scales[1], (mine,), (1,))
    products = pl.pallas_call(
        functools.partial(triangle_kernel, groups=groups, deep=deep, cols=cols),
        name="triangle",
        out_shape=jax.ShapeDtypeStruct((2 * channels, wide), BF16),
        in_specs=[SMEM, VMEM, VMEM, VMEM],
        out_specs=VMEM,
        scratch_shapes=[
            pltpu.VMEM((ranks * rows // 2, groups * LANES), BF16),
            pltpu.VMEM((ranks * rows, groups * LANES), BF16),
            pltpu.VMEM((ranks * rows // 2, groups * LANES), BF16),
        ],
    )(scale, received, both, order)
    returned = lax.all_to_all(
        products.reshape(channels, 2, -1), chips, split_axis=0, concat_axis=0, tiled=True
    )
    both = lax.all_gather(returned.reshape(2 * channels, -1), "col")
    update, new_amax = pl.pallas_call(
        functools.partial(finish_kernel, deep=deep, cols=cols),
        name="finish",
        out_shape=(
            jax.ShapeDtypeStruct((rows, channels // 2, cols), BF16),
            jax.ShapeDtypeStruct((2, channels // 2), F32),
        ),
        in_specs=[SMEM] + [VMEM] * 5,
        out_specs=(VMEM,) * 2,
        scratch_shapes=[pltpu.VMEM((channels, wide), BF16)],
    )(half, both, gating, mixer, jnp.repeat(out_gain, 2)[:, None], jnp.repeat(out_bias, 2)[:, None])
    return (jnp.transpose(update, (0, 2, 1))[None], new_amax)


def solution(mesh):
    placed = (
        P("ga", "gx", "gy", None),
        P("ga", "gx", "gy"),
        P(None, "col"),
        P(),
        P(),
        P(None, None, "col"),
        P(None, "col"),
        P(),
        P(),
        P(None, "col"),
    )
    return jax.shard_map(
        on_device,
        mesh=mesh,
        in_specs=placed,
        out_specs=(P("ga", "gx", "gy", "col"), P("ga", "col")),
        check_vma=False,
    )
```

time: 404 us -> 175 us (0.43)
  blocking collectives: 200 us -> 58.5 us
  waiting for transfers between devices: 118 us -> 59.4 us
  local copies, waits for them, and re-layouts: 39.4 us -> 8.72 us
  starting transfers between devices: 4.97 us -> 26.8 us
  Pallas kernels: 0 us -> 20.2 us
  other arithmetic: 16.5 us -> 0.03 us
  between operations: 14.3 us -> 0.71 us
  matrix products: 10.7 us -> 0 us
    all_gather x2 -> x4, blocking collectives: 200 us -> 58.5 us  [the longest x1 43.2 us: on_device(): lax.all_gather(amax_history, 'col')]
    all_gather x1 -> x0, waiting for transfers between devices: 117 us -> none  [crop_triangle(): wide_rows = lax.all_gather(right_q, 'gy', axis=2, tiled=True)]
    all_to_all x1 -> x2, waiting for transfers between devices: 0.01 us -> 59.4 us  [the longest x1 34.5 us: on_device(): lax.all_to_all(message.reshape(channels, 2, -1), chips, split_axis=0, con...]
    all_to_all x1 -> x2, starting transfers between devices: 4.84 us -> 26.8 us  [the longest x1 14.3 us: on_device(): lax.all_to_all(message.reshape(channels, 2, -1), chips, split_axis=0, con...]
    pallas_call x0 -> x4, Pallas kernels: none -> 20.2 us  [the longest x1 5.68 us: on_device(): pl.pallas_call(functools.partial(triangle_kernel, groups=groups, deep=dee...]
    all_gather x1 -> x0, local copies, waits for them, and re-layouts: 14.6 us -> none  [crop_triangle(): wide_rows = lax.all_gather(right_q, 'gy', axis=2, tiled=True)]
    transpose x1, local copies, waits for them, and re-layouts: 10.9 us -> 0.12 us  [on_device(): inverse = jnp.repeat((1.0 / scales).T, 2, axis=0)]
    dot_general x4 -> x0, matrix products: 10.7 us -> none  [the longest x1 5.11 us: crop_triangle(): jnp.einsum('cik,cjk->cij', gather_directly(left_q, 'gy', 2), panel, prefe...]
  transfers between devices with their start and end apart: 3 -> 2, of which waited for: 1 -> 2; matrix products, arithmetic and copies ran while one was open for 7% -> 1% of each run, Pallas kernels for 0% -> 3%
where the time goes in v1:
time: 175 us; the launch traced here: 174 us
  waiting for transfers between devices  59.4 us (34%)
  blocking collectives  58.5 us (33%)
  starting transfers between devices  26.8 us (15%)
  Pallas kernels  20.2 us (12%)
  local copies, waits for them, and re-layouts  8.72 us (5%)
    all_gather x1, blocking collectives, on_device(): lax.all_gather(amax_history, 'col')  43.2 us
    all_to_all x1, waiting for transfers between devices, on_device(): lax.all_to_all(message.reshape(channels, 2, -1), chips, split_axis=0, con...  34.5 us
    all_to_all x1, waiting for transfers between devices, on_device(): lax.all_to_all(products.reshape(channels, 2, -1), chips, split_axis=0, co...  24.9 us
    all_to_all x1, starting transfers between devices, on_device(): lax.all_to_all(message.reshape(channels, 2, -1), chips, split_axis=0, con...  14.3 us
    all_to_all x1, starting transfers between devices, on_device(): lax.all_to_all(products.reshape(channels, 2, -1), chips, split_axis=0, co...  12.5 us
    all_gather x1, blocking collectives, on_device(): both = lax.all_gather(received[:, edge:], 'col')  5.99 us
    all_gather x1, blocking collectives, on_device(): both = lax.all_gather(returned.reshape(2 * channels, -1), 'col')  5.76 us
    pallas_call x1, Pallas kernels, on_device(): pl.pallas_call(functools.partial(triangle_kernel, groups=groups, deep=dee...  5.68 us
  transfers between devices with their start and end apart: 2, of which 2 were waited for; matrix products, arithmetic and copies ran while one was open for 1% of the time, Pallas kernels for 3%

profile of v1, /device:TPU:65, one launch (start us, length us, event | category | flops | bytes accessed | tf_op | source)
XLA Modules:
  0.0 174.3 jit_solution(7472065773616305000)
XLA Ops:
  0.6 43.2 %all-gather.3 = f32[2,2,64]{2,1,0:T(2,128)S(1)} all-gather(f32[1,2,64]{2,1,0:T(2,128)} %bitcast.29), channel_id=2, replica_groups=mesh['ga'=2,'gx'=16,'gy'=8,'col'=2] {'col'}, dimensions={0}, use_global_device_ids=true | all-gather | bytes 1536 | tf_op jit(solution)/shard_map/all_gather | solution.py:272
  43.8 0.1 div.22
  43.9 0.1 copy.17
  44.0 3.6 %all-gather.1 = bf16[8,64,128]{2,1,0:T(8,128)(2,1)} all-gather(bf16[4,64,128]{2,1,0:T(8,128)(2,1)} %bitcast.26), channel_id=3, replica_groups=mesh['ga'=2,'gx'=16,'gy'=8,'col'=2] {'col'}, dimensions={0}, use_global_device_ids=true | all-gather | bytes 196608 | tf_op jit(solution)/shard_map/all_gather | solution.py:271
  47.6 0.7 broadcast_in_dim.18
  48.3 5.7 %project.1 = bf16[256,1664]{1,0:T(8,128)(2,1)} custom-call(s32[1]{0:T(128)} %bitcast.half_ref, bf16[40,80,128]{2,1,0:T(8,128)(2,1)} %bitcast.22, s32[40,80]{1,0:T(8,128)} %bitcast.27, bf16[2,4,64,128]{3,2,1,0:T(8,128)(2,1)} %bitcast.24, f32[256,2]{1,0:T(8,128)} %bitcast.25, f32[1,128]{1,0:T(1,128)} %bitcast.30, f32[1,128]{1,0:T(1,128)} %bitcast.32), custom_call_target="tpu_custom_call" | custom-call | tf_op jit(solution)/shard_map/project/pallas_call | solution.py:275
  54.0 3.0 %reshape.31 = bf16[128,2,1664]{2,1,0:T(2,128)(2,1)} reshape(bf16[256,1664]{1,0:T(8,128)(2,1)} %project.1) | data formatting | bytes 1703936 | tf_op jit(solution)/shard_map/reshape | solution.py:288
  57.0 14.3 %all-to-all-start = ((bf16[128,2,1664]{2,1,0:T(2,128)(2,1)}), bf16[128,2,1664]{2,1,0:T(2,128)(2,1)S(1)}, u32[]{:S(2)}, u32[]{:S(2)}) async-start(bf16[128,2,1664]{2,1,0:T(2,128)(2,1)} %reshape.31), calls=%async_computation | async-start | bytes 1703936 | tf_op jit(solution)/shard_map/all_to_all | solution.py:287
  71.3 0.1 mul.11
  71.4 0.6 constant_dynamic-slice_fusion
  72.0 5.4 %gate.1 = (f32[2,128,896]{2,1,0:T(8,128)}, bf16[128,256]{1,0:T(8,128)(2,1)}, bf16[640,1024]{1,0:T(8,128)(2,1)}) custom-call(bf16[40,80,128]{2,1,0:T(8,128)(2,1)} %bitcast.23, bf16[64,128]{1,0:T(8,128)(2,1)} %bitcast.35, bf16[64,128]{1,0:T(8,128)(2,1)} %bitcast.36, f32[1,128]{1,0:T(1,128)} %bitcast.31, f32[1,128]{1,0:T(1,128)} %bitcast.33), custom_call_target="tpu_custom_call" | custom-call | flops 20000000000 | bytes 3000000 | tf_op jit(solution)/shard_map/gate/pallas_call | solution.py:290
  77.4 34.5 %all-to-all-done = bf16[128,2,1664]{2,1,0:T(2,128)(2,1)S(1)} async-done(((bf16[128,2,1664]{2,1,0:T(2,128)(2,1)}), bf16[128,2,1664]{2,1,0:T(2,128)(2,1)S(1)}, u32[]{:S(2)}, u32[]{:S(2)}) %all-to-all-start) | async-done | bytes 852000 | tf_op jit(solution)/shard_map/all_to_all | solution.py:287
  111.9 0.3 reshape.32.own_ref
  112.2 6.0 %all-gather.2 = bf16[512,896]{1,0:T(8,128)(2,1)} all-gather(bf16[256,896]{1,0:T(8,128)(2,1)S(1)} %slice.16), channel_id=4, replica_groups=mesh['ga'=2,'gx'=16,'gy'=8,'col'=2] {'col'}, dimensions={0}, use_global_device_ids=true | all-gather | bytes 1376256 | tf_op jit(solution)/shard_map/all_gather | solution.py:305
  118.2 5.7 %triangle.1 = bf16[256,896]{1,0:T(8,128)(2,1)} custom-call(f32[1]{0:T(128)} %bitcast.3.scale_ref, bf16[256,1664]{1,0:T(8,128)(2,1)} %copy-done, bf16[2,256,896]{2,1,0:T(8,128)(2,1)} %bitcast.21, bf16[640,1024]{1,0:T(8,128)(2,1)} %get-tuple-element.7.order_ref), custom_call_target="tpu_custom_call" | custom-call | tf_op jit(solution)/shard_map/triangle/pallas_call | solution.py:308
  123.9 2.0 %reshape.33 = bf16[128,2,896]{2,1,0:T(2,128)(2,1)} reshape(bf16[256,896]{1,0:T(8,128)(2,1)} %triangle.1) | data formatting | bytes 917504 | tf_op jit(solution)/shard_map/reshape | solution.py:321
  125.9 12.5 %all-to-all-start.1 = ((bf16[128,2,896]{2,1,0:T(2,128)(2,1)}), bf16[128,2,896]{2,1,0:T(2,128)(2,1)S(1)}, u32[]{:S(2)}, u32[]{:S(2)}) async-start(bf16[128,2,896]{2,1,0:T(2,128)(2,1)} %reshape.33), calls=%async_computation.1 | async-start | bytes 917504 | tf_op jit(solution)/shard_map/all_to_all | solution.py:320
  138.4 0.1 broadcast_in_dim.21
  138.5 0.7 broadcast_in_dim_reshape.8.gain_ref
  139.3 0.8 broadcast_in_dim_reshape.9.bias_ref
  140.1 24.9 %all-to-all-done.1 = bf16[128,2,896]{2,1,0:T(2,128)(2,1)S(1)} async-done(((bf16[128,2,896]{2,1,0:T(2,128)(2,1)}), bf16[128,2,896]{2,1,0:T(2,128)(2,1)S(1)}, u32[]{:S(2)}, u32[]{:S(2)}) %all-to-all-start.1) | async-done | bytes 458784 | tf_op jit(solution)/shard_map/all_to_all | solution.py:320
  164.9 0.2 all_gather_reshape.3
  165.1 5.8 %all_gather.27.both_ref = bf16[2,256,896]{2,1,0:T(8,128)(2,1)} all-gather(bf16[1,256,896]{2,1,0:T(8,128)(2,1)S(1)} %all_gather_reshape.3), channel_id=1, replica_groups=mesh['ga'=2,'gx'=16,'gy'=8,'col'=2] {'col'}, dimensions={0}, use_global_device_ids=true | all-gather | bytes 1376256 | tf_op jit(solution)/shard_map/all_gather | solution.py:323
  170.9 3.4 %finish.1 = (bf16[40,64,80]{2,1,0:T(8,128)(2,1)}, f32[2,64]{1,0:T(2,128)}) custom-call(s32[1]{0:T(128)} %bitcast.half_ref, bf16[2,256,896]{2,1,0:T(8,128)(2,1)} %all_gather.27.both_ref, f32[2,128,896]{2,1,0:T(8,128)} %get-tuple-element.8.gating_ref, bf16[128,256]{1,0:T(8,128)(2,1)} %get-tuple-element.9.mixer_ref, f32[256,1]{1,0:T(8,128)} %broadcast_in_dim_reshape.8.gain_ref, ...), custom_call_target="tpu_custom_call" | custom-call | tf_op jit(solution)/shard_map/finish/pallas_call | solution.py:324
  (12 shorter events, 0.2 us)
Async XLA Ops:
  57.0 54.9 %all-to-all-start = ((bf16[128,2,1664]{2,1,0:T(2,128)(2,1)}), bf16[128,2,1664]{2,1,0:T(2,128)(2,1)S(1)}, u32[]{:S(2)}, u32[]{:S(2)}) async-start(bf16[128,2,1664]{2,1,0:T(2,128)(2,1)} %reshape.31), calls=%async_computation | async-start | bytes 1703936 | tf_op jit(solution)/shard_map/all_to_all | solution.py:287
  112.2 6.0 %copy-start = (bf16[256,1664]{1,0:T(8,128)(2,1)}, bf16[256,1664]{1,0:T(8,128)(2,1)S(1)}, u32[]{:S(2)}) copy-start(bf16[256,1664]{1,0:T(8,128)(2,1)S(1)} %reshape.32.own_ref) | copy-start | bytes 2555908
  123.9 14.5 %copy-start.1 = (f32[128]{0:T(128)S(1)}, f32[128]{0:T(128)}, u32[]{:S(2)}) copy-start(f32[128]{0:T(128)} %param.17) | copy-start | bytes 1540
  123.9 15.3 %copy-start.2 = (f32[128]{0:T(128)S(1)}, f32[128]{0:T(128)}, u32[]{:S(2)}) copy-start(f32[128]{0:T(128)} %param.18) | copy-start | bytes 1540
  125.9 39.0 %all-to-all-start.1 = ((bf16[128,2,896]{2,1,0:T(2,128)(2,1)}), bf16[128,2,896]{2,1,0:T(2,128)(2,1)S(1)}, u32[]{:S(2)}, u32[]{:S(2)}) async-start(bf16[128,2,896]{2,1,0:T(2,128)(2,1)} %reshape.33), calls=%async_computation.1 | async-start | bytes 917504 | tf_op jit(solution)/shard_map/all_to_all | solution.py:320

commit v2 on v1

v2 whole, which is shorter than its diff:
```python
import functools

import jax
import jax.numpy as jnp
from jax import lax
from jax.experimental import pallas as pl
from jax.experimental.pallas import tpu as pltpu
from jax.sharding import PartitionSpec as P

epsilon = 1e-05
format_limit = 448.0
LANES = 128
F32 = jnp.float32
BF16 = jnp.bfloat16


def lane_round(size):
    return -(-size // LANES) * LANES


def normed_rows(rows, gain, bias):
    average = jnp.mean(rows, axis=-1, keepdims=True)
    spread = jnp.mean(jnp.square(rows - average), axis=-1, keepdims=True)
    return ((rows - average) * lax.rsqrt(spread + epsilon) * gain + bias).astype(BF16)


def one_hot_rows(channels, parity, dtype=BF16):
    row = lax.broadcasted_iota(jnp.int32, (2 * channels, channels), 0)
    col = lax.broadcasted_iota(jnp.int32, (2 * channels, channels), 1)
    return jnp.where(row == 2 * col + parity, 1.0, 0.0).astype(dtype)


def one_hot_cols(channels, parity):
    row = lax.broadcasted_iota(jnp.int32, (channels, 2 * channels), 0)
    col = lax.broadcasted_iota(jnp.int32, (channels, 2 * channels), 1)
    return jnp.where(col == 2 * row + parity, 1.0, 0.0).astype(BF16)


def in_hbm(array):
    return pltpu.with_memory_space_constraint(array, pltpu.HBM)


def nn(left, right):
    return jnp.dot(left, right, preferred_element_type=F32)


def nt(left, right):
    return lax.dot_general(left, right, (((1,), (1,)), ((), ())), preferred_element_type=F32)


def split_parts(values):
    high = values.astype(BF16).astype(F32)
    middle = (values - high).astype(BF16).astype(F32)
    return high, middle, values - high - middle


def columns_of(rows, channels):
    parts = jnp.concatenate([*split_parts(rows), jnp.zeros_like(rows)], axis=0).astype(BF16)
    return columns_of_parts(parts, channels)


def columns_of_parts(parts, channels):
    both = (one_hot_rows(channels, 0, F32) + one_hot_rows(channels, 1, F32)).astype(BF16)
    columns = nt(both, parts)
    return columns[:, 0:2] + columns[:, 2:4] + columns[:, 4:6]


def prepare_kernel(
    half_ref,
    rep_hbm,
    mask_hbm,
    weight_hbm,
    history_hbm,
    gain_hbm,
    bias_hbm,
    packed_ref,
    near,
    far,
    masks_ref,
    rep_ref,
    mask_ref,
    weight_ref,
    history_ref,
    gain_ref,
    bias_ref,
    sems,
):
    which, outs, channels = weight_ref.shape
    held, cols = rep_ref.shape[:2]
    deep = held // 2
    span = deep * cols
    wide = near.shape[0]
    shift = span - (wide - LANES)
    half = half_ref[0]
    copies = [
        pltpu.make_async_copy(source, target, sems.at[at])
        for at, (source, target) in enumerate(
            (
                (rep_hbm.at[pl.ds(half * held, held)], rep_ref),
                (gain_hbm, gain_ref),
                (bias_hbm, bias_ref),
                (mask_hbm, mask_ref),
                (weight_hbm, weight_ref),
                (history_hbm, history_ref),
            )
        )
    ]
    for copy in copies:
        copy.start()
    near[pl.ds(span, wide - span), :] = jnp.zeros((wide - span, 2 * channels), BF16)
    far[pl.ds(0, shift), :] = jnp.zeros((shift, 2 * channels), BF16)
    far[pl.ds(shift + span, wide - span - shift), :] = jnp.zeros((wide - span - shift, 2 * channels), BF16)
    for copy in copies:
        copy.wait()
    for at in range(which):
        packed_ref[at * outs : (at + 1) * outs, :] = weight_ref[at]
    history = history_ref[...]
    parts = jnp.concatenate([*split_parts(history), jnp.zeros_like(history)], axis=0)
    parts = jnp.concatenate([parts, jnp.zeros_like(parts)], axis=1)
    parts = jnp.concatenate([parts, jnp.zeros_like(parts)], axis=0)
    packed_ref[which * outs :, :] = parts.astype(BF16)
    gain, bias = gain_ref[...], bias_ref[...]
    for part in range(2):
        for at in range(deep):
            block = normed_rows(rep_ref[part * deep + at].astype(F32), gain, bias)
            lanes = slice(part * channels, (part + 1) * channels)
            near[at * cols : (at + 1) * cols, lanes] = block
            far[shift + at * cols : shift + (at + 1) * cols, lanes] = block
    masks = mask_ref[...].astype(F32)
    masks = jnp.where(half == 0, masks[:held], masks[held:])
    pieces = [
        jnp.concatenate([masks[at : at + 1], masks[deep + at : deep + at + 1]], axis=0)
        for at in range(deep)
    ]
    zeros = jnp.zeros((2, wide - span), F32)
    mask_near = jnp.concatenate([jnp.concatenate([*pieces, zeros], axis=1)] * 4, axis=0)
    masks_ref[0] = mask_near
    masks_ref[1] = pltpu.roll(mask_near, shift, 1)


def history_parts(packed_ref, outs):
    start = packed_ref.shape[1] - 16
    pieces = [packed_ref[col, start:, :][:, :outs] for col in range(2)]
    return jnp.concatenate(pieces, axis=1)[:8]


def project_kernel(packed_ref, near, far, masks_ref, out_ref, proj, inverse_ref, *, span):
    wide, channels = near.shape[0], near.shape[1] // 2
    outs = channels // 2
    shift = span - (wide - LANES)
    inverse_ref[...] = format_limit / columns_of_parts(history_parts(packed_ref, outs), channels)
    even, odd = one_hot_rows(channels, 0), one_hot_rows(channels, 1)
    for which in range(4):
        here = pl.ds(which * outs, outs)
        weight = jnp.concatenate([packed_ref[0, here, :], packed_ref[1, here, :]], axis=0)
        weight = jnp.concatenate([nn(even, weight), nn(odd, weight)], axis=1).astype(BF16)
        proj[which] = nt(weight, (near if which < 2 else far)[...])
    mask_near = jnp.concatenate([masks_ref[0]] * 2, axis=0)
    mask_far = jnp.concatenate([masks_ref[1]] * 2, axis=0)
    lane = lax.broadcasted_iota(jnp.int32, (16, LANES), 1)
    first = shift + span - (wide - LANES)

    def step(at, carry):
        rows_at = pl.ds(pl.multiple_of(at * 16, 16), 16)
        left = mask_near * jax.nn.sigmoid(proj[1, rows_at, :]) * proj[0, rows_at, :]
        right = mask_far * jax.nn.sigmoid(proj[3, rows_at, :]) * proj[2, rows_at, :]
        left_max = jnp.max(jnp.abs(left), axis=1, keepdims=True)
        right_max = jnp.max(jnp.abs(right), axis=1, keepdims=True)
        inverse = inverse_ref[rows_at, :]
        left = jnp.clip(left * inverse[:, 0:1], -format_limit, format_limit)
        right = jnp.clip(right * inverse[:, 1:2], -format_limit, format_limit)
        edge = wide - LANES
        peers_at = pl.ds(at * 8, 8)

        def put(start, stop, values):
            out_ref[peers_at, :, start:stop] = values.astype(BF16).reshape(8, 2, stop - start)

        put(0, edge, left[:, :edge])
        put(edge, wide, left[:, edge:] + right[:, :LANES])
        put(wide, wide + edge - LANES, right[:, LANES:edge])
        last = right[:, edge:]
        for place, part in enumerate((*split_parts(left_max), *split_parts(right_max))):
            last = jnp.where(lane == first + place, part, last)
        put(wide + edge - LANES, wide + edge, last)
        return carry

    lax.fori_loop(0, 2 * channels // 16, step, 0)


def gate_kernel(
    mine_ref,
    rep_ref,
    packed_ref,
    gate_ref,
    weight_ref,
    gain_ref,
    bias_ref,
    affine_ref,
    gating_ref,
    mixer_ref,
    order_ref,
    columns_ref,
    scale_ref,
    near,
):
    rows, cols, channels = rep_ref.shape
    deep = rows // 4
    span = deep * cols
    outs = gate_ref.shape[0]
    gain, bias = gain_ref[...], bias_ref[...]
    blank = jnp.zeros((outs, channels), BF16)
    gate = gate_ref[...]
    wide_gate = jnp.concatenate(
        [jnp.concatenate([gate, blank], axis=1), jnp.concatenate([blank, gate], axis=1)], axis=0
    )
    near[span:, :] = jnp.zeros((near.shape[0] - span, 2 * channels), BF16)
    for half in range(2):
        for part in range(2):
            for at in range(deep):
                block = rep_ref[half * (2 * deep) + part * deep + at].astype(F32)
                near[at * cols : (at + 1) * cols, part * channels : (part + 1) * channels] = normed_rows(
                    block, gain, bias
                )
        gating_ref[half] = jax.nn.sigmoid(nt(wide_gate, near[...]))
    columns_ref[...] = columns_of(affine_ref[...], channels)
    parts = history_parts(packed_ref, outs).astype(F32)
    lane = lax.broadcasted_iota(jnp.int32, parts.shape, 1)
    parts = jnp.sum(jnp.where(lane == mine_ref[0], parts, 0.0), axis=1, keepdims=True)
    scales = (parts[0:2] + parts[2:4] + parts[4:6]) / format_limit
    scale_ref[...] = jnp.broadcast_to(scales[0:1] * scales[1:2], scale_ref.shape)
    weight = weight_ref[...]
    mixer_ref[0:outs, :] = nn(weight, one_hot_cols(channels, 0)).astype(BF16)
    mixer_ref[outs:, :] = nn(weight, one_hot_cols(channels, 1)).astype(BF16)
    count, lanes = order_ref.shape
    per_half = count // 2
    per_at = per_half // deep
    pairs = cols // rows
    step = 32
    for start in range(0, count, step):
        row = start + lax.broadcasted_iota(jnp.int32, (step, 1), 0)
        half_at = start // per_half
        deep_at = (start % per_half) // per_at
        block = (row - half_at * per_half - deep_at * per_at) >> 1
        part = row & 1
        target = (block // pairs) * LANES + (block % pairs) * rows + half_at * 2 * deep + part * deep + deep_at
        lane = lax.broadcasted_iota(jnp.int32, (step, lanes), 1)
        order_ref[start : start + step, :] = jnp.where(lane == target, 1.0, 0.0).astype(BF16)


def unpack_kernel(received_ref, left_ref, right_ref, flat, *, groups, deep, cols):
    rows, lanes = flat.shape
    block = rows // groups
    span = deep * cols
    for group in range(groups):
        piece = received_ref[group * block // 2 : (group + 1) * block // 2]
        flat[group * block : (group + 1) * block, :] = piece.reshape(block, lanes)

    def window(group, start):
        base = start // LANES * LANES
        stop = -(-(start + cols) // LANES) * LANES
        return flat[group * block : (group + 1) * block, base:stop][:, start - base : start - base + cols]

    for at in range(deep):
        place = pl.ds(at * block, block)
        left_ref[place, :] = jnp.concatenate([window(g, at * cols) for g in range(groups)], axis=1)
        right_ref[place, :] = jnp.concatenate([window(g, span + at * cols) for g in range(groups)], axis=1)
    parts = flat[:, lanes - LANES :].astype(F32)
    total = parts + pltpu.roll(parts, LANES - 1, 1) + pltpu.roll(parts, LANES - 2, 1)
    best = jnp.max(jnp.max(total.reshape(rows // 8, 8, LANES), axis=0), axis=0, keepdims=True)
    best = jnp.concatenate([*split_parts(best), jnp.zeros((13, LANES), F32)], axis=0).astype(BF16)
    right_ref[deep * block :, :] = jnp.concatenate(
        [best, jnp.zeros((16, groups * cols - LANES), BF16)], axis=1
    )


def triangle_kernel(scale_ref, left_ref, both_ref, order_ref, out_ref, moved, *, groups, deep, cols):
    count = left_ref.shape[0]
    block = count // deep
    span = deep * cols
    scale = scale_ref[0:1, 0:1]
    total = None
    best = None
    for other in range(2):
        products = nt(left_ref[...], both_ref[other, :count, :]) * scale
        turned = nn(products.astype(BF16), order_ref[other * count : (other + 1) * count, :])
        total = turned if total is None else total + turned
        parts = both_ref[other, count:, :LANES].astype(F32)
        parts = parts[0:1] + parts[1:2] + parts[2:3]
        best = parts if best is None else jnp.maximum(best, parts)
    moved[...] = total.astype(BF16)
    lane = lax.broadcasted_iota(jnp.int32, (8, LANES), 1)
    first = 2 * span % LANES
    goal = span % LANES
    best = jnp.broadcast_to(best, (8, LANES))
    tail = jnp.zeros((8, LANES), F32)
    for place, part in enumerate(split_parts(best)):
        turned = pltpu.roll(part, (goal + place - first) % LANES, 1)
        tail = jnp.where((lane == goal + place) | (lane == goal + place + 3), turned, tail)
    tail = jnp.broadcast_to(tail[0:1, goal:], (block, LANES - goal)).astype(BF16)
    for group in range(groups):
        pieces = [
            moved[at * block : (at + 1) * block, group * LANES : group * LANES + cols] for at in range(deep)
        ]
        pieces = jnp.concatenate([*pieces, tail], axis=1)
        out_ref[group * block // 2 : (group + 1) * block // 2] = pieces.reshape(block // 2, 2, -1)


def finish_kernel(
    half_ref, both_ref, gating_ref, mixer_ref, columns_ref, update_ref, amax_ref, mixed, *, deep, cols
):
    rows, wide = both_ref.shape[1:]
    channels = rows // 2
    outs = update_ref.shape[1]
    span = deep * cols
    gain, bias = columns_ref[:, 0:1], columns_ref[:, 1:2]
    mixer = mixer_ref[...]

    def per_part(values):
        total = jnp.sum(values, axis=0)
        total = total + pltpu.roll(total, 4, 0)
        total = total + pltpu.roll(total, 2, 0)
        return total * (1.0 / channels)

    for half in range(2):
        for start in range(0, wide, LANES):
            values = both_ref[half, :, start : start + LANES].astype(F32).reshape(rows // 8, 8, LANES)
            values = values - per_part(values)[None]
            spread = per_part(jnp.square(values))
            values = (values * lax.rsqrt(spread + epsilon)[None]).reshape(rows, LANES)
            tnorm = (values * gain + bias).astype(BF16)
            mixing = nn(mixer, tnorm)
            mixed[:, start : start + LANES] = (gating_ref[half, :, start : start + LANES] * mixing).astype(BF16)
        for part in range(2):
            for at in range(deep):
                place = half * 2 * deep + part * deep + at
                update_ref[place] = mixed[part * outs : (part + 1) * outs, at * cols : (at + 1) * cols]
    last = both_ref[0, :, wide - LANES :]
    row = lax.broadcasted_iota(jnp.int32, (rows, outs), 0)
    col = lax.broadcasted_iota(jnp.int32, (rows, outs), 1)
    chosen = jnp.where(row == 2 * (col + half_ref[0] * outs), 1.0, 0.0).astype(BF16)
    sums = lax.dot_general(last, chosen, (((0,), (0,)), ((), ())), preferred_element_type=F32)
    goal = span % LANES
    amax_ref[0:1, :] = sums[goal : goal + 1] + sums[goal + 1 : goal + 2] + sums[goal + 2 : goal + 3]
    amax_ref[1:2, :] = sums[goal + 3 : goal + 4] + sums[goal + 4 : goal + 5] + sums[goal + 5 : goal + 6]


VMEM = pl.BlockSpec(memory_space=pltpu.VMEM)
HBM = pl.BlockSpec(memory_space=pltpu.HBM)
SMEM = pl.BlockSpec(memory_space=pltpu.SMEM)
GRANT = pltpu.CompilerParams(vmem_limit_bytes=24 * 2**20)


def on_device(
    pair_rep,
    pair_mask,
    amax_history,
    in_gain,
    in_bias,
    proj_weight,
    gate_weight,
    out_gain,
    out_bias,
    out_weight,
):
    rows, cols, channels = pair_rep.shape[1:]
    deep = rows // 4
    span = deep * cols
    wide = lane_round(span)
    groups, ranks = lax.axis_size("gy"), lax.axis_size("gx")
    chips = ("gy", "gx")
    assert groups * ranks == channels and lax.axis_size("col") == 2
    half = lax.axis_index("col").reshape(1).astype(jnp.int32)
    rep = pair_rep[0]
    gain, bias = in_gain[None, :], in_bias[None, :]

    packed, near, far, masks = pl.pallas_call(
        prepare_kernel,
        name="prepare",
        out_shape=(
            jax.ShapeDtypeStruct((2 * channels + 16, channels), BF16),
            jax.ShapeDtypeStruct((wide, 2 * channels), BF16),
            jax.ShapeDtypeStruct((wide, 2 * channels), BF16),
            jax.ShapeDtypeStruct((2, 8, wide), F32),
        ),
        in_specs=[SMEM] + [HBM] * 6,
        out_specs=(VMEM,) * 4,
        scratch_shapes=[
            pltpu.VMEM((rows // 2, cols, channels), BF16),
            pltpu.VMEM((rows, cols), jnp.int32),
            pltpu.VMEM((4, channels // 2, channels), BF16),
            pltpu.VMEM((2, channels // 2), F32),
            pltpu.VMEM((1, channels), F32),
            pltpu.VMEM((1, channels), F32),
            pltpu.SemaphoreType.DMA((6,)),
        ],
        compiler_params=GRANT,
    )(half, *map(in_hbm, (rep, pair_mask[0], jnp.transpose(proj_weight, (1, 2, 0)), amax_history, gain, bias)))
    packed = lax.all_gather(packed, "col")
    message = pl.pallas_call(
        functools.partial(project_kernel, span=span),
        name="project",
        out_shape=jax.ShapeDtypeStruct((channels, 2, 2 * wide - LANES), BF16),
        in_specs=[VMEM] * 4,
        out_specs=VMEM,
        scratch_shapes=[
            pltpu.VMEM((4, 2 * channels, wide), F32),
            pltpu.VMEM((2 * channels, 2), F32),
        ],
        compiler_params=GRANT,
    )(packed, near, far, masks)
    received = lax.all_to_all(message, chips, split_axis=0, concat_axis=0, tiled=True)
    mine = lax.axis_index(chips).reshape(1).astype(jnp.int32)
    gating, mixer, order, columns, scale = pl.pallas_call(
        gate_kernel,
        name="gate",
        out_shape=(
            jax.ShapeDtypeStruct((2, channels, wide), F32),
            jax.ShapeDtypeStruct((channels, 2 * channels), BF16),
            jax.ShapeDtypeStruct((ranks * rows, groups * LANES), BF16),
            jax.ShapeDtypeStruct((2 * channels, 2), F32),
            jax.ShapeDtypeStruct((8, LANES), F32),
        ),
        in_specs=[SMEM] + [VMEM] * 7,
        out_specs=(VMEM,) * 5,
        scratch_shapes=[pltpu.VMEM((wide, 2 * channels), BF16)],
        compiler_params=GRANT,
        cost_estimate=pl.CostEstimate(flops=20_000_000_000, bytes_accessed=3_000_000, transcendentals=0),
    )(mine, rep, packed, gate_weight.T, out_weight.T, gain, bias, jnp.stack([out_gain, out_bias]))
    count = ranks * rows // 2
    left, right = pl.pallas_call(
        functools.partial(unpack_kernel, groups=groups, deep=deep, cols=cols),
        name="unpack",
        out_shape=(
            jax.ShapeDtypeStruct((count, groups * cols), BF16),
            jax.ShapeDtypeStruct((count + 16, groups * cols), BF16),
        ),
        in_specs=[VMEM],
        out_specs=(VMEM,) * 2,
        scratch_shapes=[pltpu.VMEM((2 * channels, 2 * wide - LANES), BF16)],
        compiler_params=GRANT,
    )(received)
    both = lax.all_gather(right, "col")
    products = pl.pallas_call(
        functools.partial(triangle_kernel, groups=groups, deep=deep, cols=cols),
        name="triangle",
        out_shape=jax.ShapeDtypeStruct((channels, 2, wide), BF16),
        in_specs=[VMEM] * 4,
        out_specs=VMEM,
        scratch_shapes=[pltpu.VMEM((count, groups * LANES), BF16)],
        compiler_params=GRANT,
    )(scale, left, both, order)
    returned = lax.all_to_all(products, chips, split_axis=0, concat_axis=0, tiled=True)
    both = lax.all_gather(returned.reshape(2 * channels, -1), "col")
    update, new_amax = pl.pallas_call(
        functools.partial(finish_kernel, deep=deep, cols=cols),
        name="finish",
        out_shape=(
            jax.ShapeDtypeStruct((rows, channels // 2, cols), BF16),
            jax.ShapeDtypeStruct((2, channels // 2), F32),
        ),
        in_specs=[SMEM] + [VMEM] * 4,
        out_specs=(VMEM,) * 2,
        scratch_shapes=[pltpu.VMEM((channels, wide), BF16)],
        compiler_params=GRANT,
    )(half, both, gating, mixer, columns)
    return (jnp.transpose(update, (0, 2, 1))[None], new_amax)


def solution(mesh):
    placed = (
        P("ga", "gx", "gy", None),
        P("ga", "gx", "gy"),
        P(None, "col"),
        P(),
        P(),
        P(None, None, "col"),
        P(None, "col"),
        P(),
        P(),
        P(None, "col"),
    )
    return jax.shard_map(
        on_device,
        mesh=mesh,
        in_specs=placed,
        out_specs=(P("ga", "gx", "gy", "col"), P("ga", "col")),
        check_vma=False,
    )
```

time: 175 us -> 160 us (0.914)
  blocking collectives: 58.5 us -> 93.5 us
  waiting for transfers between devices: 59.4 us -> 35.9 us
  starting transfers between devices: 26.8 us -> 14.4 us
  local copies, waits for them, and re-layouts: 8.72 us -> 1.34 us
  Pallas kernels: 20.2 us -> 14.1 us
    all_to_all x0 -> x1, blocking collectives: none -> 38.8 us  [on_device(): lax.all_to_all(products, chips, split_axis=0, concat_axis=0, tiled=True)]
    all_to_all x2 -> x1, waiting for transfers between devices: 59.4 us -> 35.9 us  [on_device(): lax.all_to_all(message, chips, split_axis=0, concat_axis=0, tiled=True)]
    all_to_all x2 -> x1, starting transfers between devices: 26.8 us -> 14.4 us  [on_device(): lax.all_to_all(message, chips, split_axis=0, concat_axis=0, tiled=True)]
    reshape x3 -> x0, local copies, waits for them, and re-layouts: 5.28 us -> none  [the longest x1 2.97 us: on_device(): message.reshape(channels, 2, -1)]
    pallas_call x1, Pallas kernels: 5.68 us -> 1.54 us  [on_device(): pl.pallas_call(functools.partial(triangle_kernel, groups=groups, deep=dee...]
    all_gather x3 -> x2, blocking collectives: 52.7 us -> 49.1 us  [the longest x1 43 us: on_device(): packed = lax.all_gather(packed, 'col')]
    pallas_call x1, Pallas kernels: 5.38 us -> 3.19 us  [on_device(): pl.pallas_call(gate_kernel, name='gate', out_shape=(jax.ShapeDtypeStruct(...]
    pallas_call x1 -> x3, Pallas kernels: 5.67 us -> 7.33 us  [the longest x1 4.19 us: on_device(): pl.pallas_call(functools.partial(project_kernel, span=span), name='projec...]
  transfers between devices with their start and end apart: 2 -> 1, of which waited for: 2 -> 1; matrix products, arithmetic and copies ran while one was open for 1% -> 0% of each run, Pallas kernels for 3% -> 2%
where the time goes in v2:
time: 160 us
  blocking collectives  93.5 us (58%)
  waiting for transfers between devices  35.9 us (22%)
  starting transfers between devices  14.4 us (9%)
  Pallas kernels  14.1 us (9%)
    all_gather x1, blocking collectives, on_device(): packed = lax.all_gather(packed, 'col')  43 us
    all_to_all x1, blocking collectives, on_device(): lax.all_to_all(products, chips, split_axis=0, concat_axis=0, tiled=True)  38.8 us
    all_to_all x1, waiting for transfers between devices, on_device(): lax.all_to_all(message, chips, split_axis=0, concat_axis=0, tiled=True)  35.9 us
    all_to_all x1, starting transfers between devices, on_device(): lax.all_to_all(message, chips, split_axis=0, concat_axis=0, tiled=True)  14.4 us
    all_gather x1, blocking collectives, on_device(): both = lax.all_gather(right, 'col')  6.06 us
    all_gather x1, blocking collectives, on_device(): both = lax.all_gather(returned.reshape(2 * channels, -1), 'col')  5.63 us
    pallas_call x1, Pallas kernels, on_device(): pl.pallas_call(functools.partial(project_kernel, span=span), name='projec...  4.19 us
  transfers between devices with their start and end apart: 1, of which 1 were waited for; matrix products, arithmetic and copies ran while one was open for 0% of the time, Pallas kernels for 2%

profile of v2, /device:TPU:65, one launch (start us, length us, event | category | flops | bytes accessed | tf_op | source)
XLA Modules:
  0.0 160.1 jit_solution(7258608725690436376)
XLA Ops:
  0.6 2.5 %prepare.1 = (bf16[272,128]{1,0:T(8,128)(2,1)S(1)}, bf16[896,256]{1,0:T(8,128)(2,1)S(1)}, bf16[896,256]{1,0:T(8,128)(2,1)S(1)}, f32[2,8,896]{2,1,0:T(8,128)S(1)}) custom-call(s32[1]{0:T(128)} %bitcast.half_ref, bf16[40,80,128]{2,1,0:T(8,128)(2,1)} %bitcast.17, s32[40,80]{1,0:T(8,128)} %bitcast.28, bf16[4,64,128]{2,1,0:T(8,128)(2,1)} %bitcast.27, ...), custom_call_target="tpu_custom_call" | custom-call | tf_op jit(solution)/shard_map/prepare/pallas_call | solution.py:376
  3.2 43.0 %all-gather = bf16[544,128]{1,0:T(8,128)(2,1)S(1)} all-gather(bf16[272,128]{1,0:T(8,128)(2,1)S(1)} %get-tuple-element.15), channel_id=2, replica_groups=mesh['ga'=2,'gx'=16,'gy'=8,'col'=2] {'col'}, dimensions={0}, use_global_device_ids=true | all-gather | bytes 208896 | tf_op jit(solution)/shard_map/all_gather | solution.py:398
  46.2 4.2 %project.1 = bf16[128,2,1664]{2,1,0:T(2,128)(2,1)} custom-call(bf16[2,272,128]{2,1,0:T(8,128)(2,1)S(1)} %bitcast.19, bf16[896,256]{1,0:T(8,128)(2,1)S(1)} %get-tuple-element.17.near, bf16[896,256]{1,0:T(8,128)(2,1)S(1)} %get-tuple-element.18.far, f32[2,8,896]{2,1,0:T(8,128)S(1)} %get-tuple-element.19.masks_ref), custom_call_target="tpu_custom_call" | custom-call | tf_op jit(solution)/shard_map/project/pallas_call | solution.py:399
  50.4 0.0 copy-start.6
  50.4 0.0 copy-start.3
  50.4 0.0 copy-start.4
  50.4 14.4 %all-to-all-start = ((bf16[128,2,1664]{2,1,0:T(2,128)(2,1)}), bf16[128,2,1664]{2,1,0:T(2,128)(2,1)S(1)}, u32[]{:S(2)}, u32[]{:S(2)}) async-start(bf16[128,2,1664]{2,1,0:T(2,128)(2,1)} %project.1), calls=%async_computation | async-start | bytes 1703936 | tf_op jit(solution)/shard_map/all_to_all | solution.py:411
  64.9 0.0 copy-done.5
  64.9 0.0 copy-done.6
  64.9 0.0 copy-done.1
  64.9 0.0 copy-done.2
  65.0 0.0 copy-done.3
  65.0 0.0 copy-done.4
  65.0 0.0 copy-start
  65.0 1.1 copy-done
  66.1 3.2 %gate.1 = (f32[2,128,896]{2,1,0:T(8,128)S(1)}, bf16[128,256]{1,0:T(8,128)(2,1)S(1)}, bf16[640,1024]{1,0:T(8,128)(2,1)S(1)}, f32[256,2]{1,0:T(8,128)S(1)}, f32[8,128]{1,0:T(8,128)S(1)}) custom-call(s32[1]{0:T(128)} %bitcast.1.mine_ref, bf16[40,80,128]{2,1,0:T(8,128)(2,1)S(1)} %bitcast.18, bf16[2,272,128]{2,1,0:T(8,128)(2,1)S(1)} %bitcast.20, ...), custom_call_target="tpu_custom_call" | custom-call | flops 20000000000 | bytes 3000000 | tf_op jit(solution)/shard_map/gate/pallas_call | solution.py:413
  69.3 35.9 %all-to-all-done.received_ref = bf16[128,2,1664]{2,1,0:T(2,128)(2,1)S(1)} async-done(((bf16[128,2,1664]{2,1,0:T(2,128)(2,1)}), bf16[128,2,1664]{2,1,0:T(2,128)(2,1)S(1)}, u32[]{:S(2)}, u32[]{:S(2)}) %all-to-all-start) | async-done | bytes 852000 | tf_op jit(solution)/shard_map/all_to_all | solution.py:411
  105.2 0.6 unpack.1
  105.8 6.1 %all-gather.1 = bf16[672,640]{1,0:T(8,128)(2,1)S(1)} all-gather(bf16[336,640]{1,0:T(8,128)(2,1)S(1)} %get-tuple-element.21), channel_id=3, replica_groups=mesh['ga'=2,'gx'=16,'gy'=8,'col'=2] {'col'}, dimensions={0}, use_global_device_ids=true | all-gather | bytes 1290240 | tf_op jit(solution)/shard_map/all_gather | solution.py:442
  111.9 1.5 triangle.1
  113.4 38.8 %all_to_all.10 = bf16[128,2,896]{2,1,0:T(2,128)(2,1)S(1)} all-to-all(bf16[128,2,896]{2,1,0:T(2,128)(2,1)S(1)} %triangle.1), channel_id=1, replica_groups=mesh['ga'=2,'gx'=16,'gy'=8,'col'=2] {'gy','gx'}, dimensions={0} | all-to-all | bytes 917504 | tf_op jit(solution)/shard_map/all_to_all | solution.py:452
  152.2 0.2 all_gather_reshape.3
  152.4 5.6 %all_gather.19.both_ref = bf16[2,256,896]{2,1,0:T(8,128)(2,1)S(1)} all-gather(bf16[1,256,896]{2,1,0:T(8,128)(2,1)S(1)} %all_gather_reshape.3), channel_id=1, replica_groups=mesh['ga'=2,'gx'=16,'gy'=8,'col'=2] {'col'}, dimensions={0}, use_global_device_ids=true | all-gather | bytes 1376256 | tf_op jit(solution)/shard_map/all_gather | solution.py:453
  158.0 2.0 %finish.1 = (bf16[40,64,80]{2,1,0:T(8,128)(2,1)}, f32[2,64]{1,0:T(2,128)}) custom-call(s32[1]{0:T(128)} %bitcast.half_ref, bf16[2,256,896]{2,1,0:T(8,128)(2,1)S(1)} %all_gather.19.both_ref, f32[2,128,896]{2,1,0:T(8,128)S(1)} %get-tuple-element.23.gating_ref, bf16[128,256]{1,0:T(8,128)(2,1)S(1)} %get-tuple-element.24.mixer_ref, ...), custom_call_target="tpu_custom_call" | custom-call | tf_op jit(solution)/shard_map/finish/pallas_call | solution.py:454
  (4 shorter events, 0.0 us)
Async XLA Ops:
  50.4 14.5 %copy-start.5 = (f32[128]{0:T(128)S(1)}, f32[128]{0:T(128)}, u32[]{:S(2)}) copy-start(f32[128]{0:T(128)} %param.18) | copy-start | bytes 1540
  50.4 14.5 %copy-start.6 = (f32[128]{0:T(128)S(1)}, f32[128]{0:T(128)}, u32[]{:S(2)}) copy-start(f32[128]{0:T(128)} %param.17) | copy-start | bytes 1540
  50.4 14.5 %copy-start.1 = (f32[128]{0:T(128)S(1)}, f32[128]{0:T(128)}, u32[]{:S(2)}) copy-start(f32[128]{0:T(128)} %param.13) | copy-start | bytes 1540
  50.4 14.5 %copy-start.2 = (f32[128]{0:T(128)S(1)}, f32[128]{0:T(128)}, u32[]{:S(2)}) copy-start(f32[128]{0:T(128)} %param.14) | copy-start | bytes 1540
  50.4 14.5 %copy-start.3 = (bf16[128,64]{0,1:T(8,128)(2,1)S(1)}, bf16[128,64]{0,1:T(8,128)(2,1)}, u32[]{:S(2)}) copy-start(bf16[128,64]{0,1:T(8,128)(2,1)} %param.16) | copy-start | bytes 49156
  50.4 14.5 %copy-start.4 = (bf16[128,64]{0,1:T(8,128)(2,1)S(1)}, bf16[128,64]{0,1:T(8,128)(2,1)}, u32[]{:S(2)}) copy-start(bf16[128,64]{0,1:T(8,128)(2,1)} %param.19) | copy-start | bytes 49156
  50.4 54.8 %all-to-all-start = ((bf16[128,2,1664]{2,1,0:T(2,128)(2,1)}), bf16[128,2,1664]{2,1,0:T(2,128)(2,1)S(1)}, u32[]{:S(2)}, u32[]{:S(2)}) async-start(bf16[128,2,1664]{2,1,0:T(2,128)(2,1)} %project.1), calls=%async_computation | async-start | bytes 1703936 | tf_op jit(solution)/shard_map/all_to_all | solution.py:411
  65.0 1.1 copy-start

commit v3 on v2

--- a/solution.py
+++ b/solution.py
@@ -96,7 +96,8 @@
         pltpu.make_async_copy(source, target, sems.at[at])
         for at, (source, target) in enumerate(
             (
-                (rep_hbm.at[pl.ds(half * held, held)], rep_ref),
+                (rep_hbm.at[pl.ds(half * held, deep)], rep_ref.at[pl.ds(0, deep)]),
+                (rep_hbm.at[pl.ds(half * held + deep, deep)], rep_ref.at[pl.ds(deep, deep)]),
                 (gain_hbm, gain_ref),
                 (bias_hbm, bias_ref),
                 (mask_hbm, mask_ref),
@@ -110,7 +111,7 @@
     near[pl.ds(span, wide - span), :] = jnp.zeros((wide - span, 2 * channels), BF16)
     far[pl.ds(0, shift), :] = jnp.zeros((shift, 2 * channels), BF16)
     far[pl.ds(shift + span, wide - span - shift), :] = jnp.zeros((wide - span - shift, 2 * channels), BF16)
-    for copy in copies:
+    for copy in copies[2:]:
         copy.wait()
     for at in range(which):
         packed_ref[at * outs : (at + 1) * outs, :] = weight_ref[at]
@@ -121,6 +122,7 @@
     packed_ref[which * outs :, :] = parts.astype(BF16)
     gain, bias = gain_ref[...], bias_ref[...]
     for part in range(2):
+        copies[part].wait()
         for at in range(deep):
             block = normed_rows(rep_ref[part * deep + at].astype(F32), gain, bias)
             lanes = slice(part * channels, (part + 1) * channels)
@@ -144,7 +146,7 @@
     return jnp.concatenate(pieces, axis=1)[:8]
 
 
-def project_kernel(packed_ref, near, far, masks_ref, out_ref, proj, inverse_ref, *, span):
+def project_kernel(packed_ref, near, far, masks_ref, out_hbm, proj, inverse_ref, out_ref, sems, *, span):
     wide, channels = near.shape[0], near.shape[1] // 2
     outs = channels // 2
     shift = span - (wide - LANES)
@@ -182,9 +184,19 @@
         for place, part in enumerate((*split_parts(left_max), *split_parts(right_max))):
             last = jnp.where(lane == first + place, part, last)
         put(wide + edge - LANES, wide + edge, last)
+        sent(at).start()
         return carry
 
-    lax.fori_loop(0, 2 * channels // 16, step, 0)
+    def sent(at):
+        peers_at = pl.ds(at * 8, 8)
+        return pltpu.make_async_copy(out_ref.at[peers_at], out_hbm.at[peers_at], sems.at[at])
+
+    def settle(at, carry):
+        sent(at).wait()
+        return carry
+
+    lax.fori_loop(0, channels // 8, step, 0)
+    lax.fori_loop(0, channels // 8, settle, 0)
 
 
 def gate_kernel(
@@ -306,7 +318,7 @@
 
 
 def finish_kernel(
-    half_ref, both_ref, gating_ref, mixer_ref, columns_ref, update_ref, amax_ref, mixed, *, deep, cols
+    half_ref, both_ref, gating_ref, mixer_ref, columns_ref, update_hbm, amax_ref, mixed, update_ref, sems, *, deep, cols
 ):
     rows, wide = both_ref.shape[1:]
     channels = rows // 2
@@ -314,6 +326,10 @@
     span = deep * cols
     gain, bias = columns_ref[:, 0:1], columns_ref[:, 1:2]
     mixer = mixer_ref[...]
+
+    def sent(at):
+        place = pl.ds(at * deep, deep)
+        return pltpu.make_async_copy(update_ref.at[place], update_hbm.at[place], sems.at[at])
 
     def per_part(values):
         total = jnp.sum(values, axis=0)
@@ -334,6 +350,7 @@
             for at in range(deep):
                 place = half * 2 * deep + part * deep + at
                 update_ref[place] = mixed[part * outs : (part + 1) * outs, at * cols : (at + 1) * cols]
+            sent(2 * half + part).start()
     last = both_ref[0, :, wide - LANES :]
     row = lax.broadcasted_iota(jnp.int32, (rows, outs), 0)
     col = lax.broadcasted_iota(jnp.int32, (rows, outs), 1)
@@ -342,6 +359,8 @@
     goal = span % LANES
     amax_ref[0:1, :] = sums[goal : goal + 1] + sums[goal + 1 : goal + 2] + sums[goal + 2 : goal + 3]
     amax_ref[1:2, :] = sums[goal + 3 : goal + 4] + sums[goal + 4 : goal + 5] + sums[goal + 5 : goal + 6]
+    for at in range(4):
+        sent(at).wait()
 
 
 VMEM = pl.BlockSpec(memory_space=pltpu.VMEM)
@@ -391,7 +410,7 @@
             pltpu.VMEM((2, channels // 2), F32),
             pltpu.VMEM((1, channels), F32),
             pltpu.VMEM((1, channels), F32),
-            pltpu.SemaphoreType.DMA((6,)),
+            pltpu.SemaphoreType.DMA((7,)),
         ],
         compiler_params=GRANT,
     )(half, *map(in_hbm, (rep, pair_mask[0], jnp.transpose(proj_weight, (1, 2, 0)), amax_history, gain, bias)))
@@ -399,12 +418,14 @@
     message = pl.pallas_call(
         functools.partial(project_kernel, span=span),
         name="project",
-        out_shape=jax.ShapeDtypeStruct((channels, 2, 2 * wide - LANES), BF16),
+        out_shape=pltpu.HBM((channels, 2, 2 * wide - LANES), BF16),
         in_specs=[VMEM] * 4,
-        out_specs=VMEM,
+        out_specs=HBM,
         scratch_shapes=[
             pltpu.VMEM((4, 2 * channels, wide), F32),
             pltpu.VMEM((2 * channels, 2), F32),
+            pltpu.VMEM((channels, 2, 2 * wide - LANES), BF16),
+            pltpu.SemaphoreType.DMA((channels // 8,)),
         ],
         compiler_params=GRANT,
     )(packed, near, far, masks)
@@ -455,12 +476,16 @@
         functools.partial(finish_kernel, deep=deep, cols=cols),
         name="finish",
         out_shape=(
-            jax.ShapeDtypeStruct((rows, channels // 2, cols), BF16),
+            pltpu.HBM((rows, channels // 2, cols), BF16),
             jax.ShapeDtypeStruct((2, channels // 2), F32),
         ),
         in_specs=[SMEM] + [VMEM] * 4,
-        out_specs=(VMEM,) * 2,
-        scratch_shapes=[pltpu.VMEM((channels, wide), BF16)],
+        out_specs=(HBM, VMEM),
+        scratch_shapes=[
+            pltpu.VMEM((channels, wide), BF16),
+            pltpu.VMEM((rows, channels // 2, cols), BF16),
+            pltpu.SemaphoreType.DMA((4,)),
+        ],
         compiler_params=GRANT,
     )(half, both, gating, mixer, columns)
     return (jnp.transpose(update, (0, 2, 1))[None], new_amax)

time: 160 us -> 161 us (level)
  no operation moved by 1% of the time
where the time goes in v3:
time: 161 us; the launch traced here: 160 us
  blocking collectives  93.5 us (58%)
  waiting for transfers between devices  35.9 us (22%)
  starting transfers between devices  14.4 us (9%)
  Pallas kernels  14.1 us (9%)
    all_gather x1, blocking collectives, on_device(): packed = lax.all_gather(packed, 'col')  43 us
    all_to_all x1, blocking collectives, on_device(): lax.all_to_all(products, chips, split_axis=0, concat_axis=0, tiled=True)  38.8 us
    all_to_all x1, waiting for transfers between devices, on_device(): lax.all_to_all(message, chips, split_axis=0, concat_axis=0, tiled=True)  35.9 us
    all_to_all x1, starting transfers between devices, on_device(): lax.all_to_all(message, chips, split_axis=0, concat_axis=0, tiled=True)  14.4 us
    all_gather x1, blocking collectives, on_device(): both = lax.all_gather(right, 'col')  6.06 us
    all_gather x1, blocking collectives, on_device(): both = lax.all_gather(returned.reshape(2 * channels, -1), 'col')  5.63 us
    pallas_call x1, Pallas kernels, on_device(): pl.pallas_call(functools.partial(project_kernel, span=span), name='projec...  4.05 us
  transfers between devices with their start and end apart: 1, of which 1 were waited for; matrix products, arithmetic and copies ran while one was open for 0% of the time, Pallas kernels for 2%

profile of v3, /device:TPU:65, one launch (start us, length us, event | category | flops | bytes accessed | tf_op | source)
XLA Modules:
  0.0 160.2 jit_solution(15976343315819904032)
XLA Ops:
  0.6 2.2 %prepare.1 = (bf16[272,128]{1,0:T(8,128)(2,1)S(1)}, bf16[896,256]{1,0:T(8,128)(2,1)S(1)}, bf16[896,256]{1,0:T(8,128)(2,1)S(1)}, f32[2,8,896]{2,1,0:T(8,128)S(1)}) custom-call(s32[1]{0:T(128)} %bitcast.half_ref, bf16[40,80,128]{2,1,0:T(8,128)(2,1)} %bitcast.17, s32[40,80]{1,0:T(8,128)} %bitcast.28, bf16[4,64,128]{2,1,0:T(8,128)(2,1)} %bitcast.27, ...), custom_call_target="tpu_custom_call" | custom-call | tf_op jit(solution)/shard_map/prepare/pallas_call | solution.py:395
  2.9 43.0 %all-gather = bf16[544,128]{1,0:T(8,128)(2,1)S(1)} all-gather(bf16[272,128]{1,0:T(8,128)(2,1)S(1)} %get-tuple-element.15), channel_id=2, replica_groups=mesh['ga'=2,'gx'=16,'gy'=8,'col'=2] {'col'}, dimensions={0}, use_global_device_ids=true | all-gather | bytes 208896 | tf_op jit(solution)/shard_map/all_gather | solution.py:417
  45.9 4.0 %project.1 = bf16[128,2,1664]{2,1,0:T(2,128)(2,1)} custom-call(bf16[2,272,128]{2,1,0:T(8,128)(2,1)S(1)} %bitcast.19, bf16[896,256]{1,0:T(8,128)(2,1)S(1)} %get-tuple-element.17.near, bf16[896,256]{1,0:T(8,128)(2,1)S(1)} %get-tuple-element.18.far, f32[2,8,896]{2,1,0:T(8,128)S(1)} %get-tuple-element.19.masks_ref), custom_call_target="tpu_custom_call" | custom-call | tf_op jit(solution)/shard_map/project/pallas_call | solution.py:418
  50.0 0.0 copy-start.5
  50.0 0.0 copy-start.6
  50.0 0.0 copy-start.1
  50.0 0.0 copy-start.2
  50.0 0.0 copy-start.3
  50.0 0.0 copy-start.4
  50.0 14.4 %all-to-all-start = ((bf16[128,2,1664]{2,1,0:T(2,128)(2,1)}), bf16[128,2,1664]{2,1,0:T(2,128)(2,1)S(1)}, u32[]{:S(2)}, u32[]{:S(2)}) async-start(bf16[128,2,1664]{2,1,0:T(2,128)(2,1)} %project.1), calls=%async_computation | async-start | bytes 1703936 | tf_op jit(solution)/shard_map/all_to_all | solution.py:432
  64.5 0.0 copy-done.5
  64.5 0.0 copy-done.6
  64.5 0.0 copy-done.1
  64.6 0.0 copy-start
  64.6 1.1 copy-done
  65.7 3.2 %gate.1 = (f32[2,128,896]{2,1,0:T(8,128)S(1)}, bf16[128,256]{1,0:T(8,128)(2,1)S(1)}, bf16[640,1024]{1,0:T(8,128)(2,1)S(1)}, f32[256,2]{1,0:T(8,128)S(1)}, f32[8,128]{1,0:T(8,128)S(1)}) custom-call(s32[1]{0:T(128)} %bitcast.1.mine_ref, bf16[40,80,128]{2,1,0:T(8,128)(2,1)S(1)} %bitcast.18, bf16[2,272,128]{2,1,0:T(8,128)(2,1)S(1)} %bitcast.20, ...), custom_call_target="tpu_custom_call" | custom-call | flops 20000000000 | bytes 3000000 | tf_op jit(solution)/shard_map/gate/pallas_call | solution.py:434
  68.9 35.9 %all-to-all-done.received_ref = bf16[128,2,1664]{2,1,0:T(2,128)(2,1)S(1)} async-done(((bf16[128,2,1664]{2,1,0:T(2,128)(2,1)}), bf16[128,2,1664]{2,1,0:T(2,128)(2,1)S(1)}, u32[]{:S(2)}, u32[]{:S(2)}) %all-to-all-start) | async-done | bytes 852000 | tf_op jit(solution)/shard_map/all_to_all | solution.py:432
  104.8 0.6 unpack.1
  105.4 6.1 %all-gather.1 = bf16[672,640]{1,0:T(8,128)(2,1)S(1)} all-gather(bf16[336,640]{1,0:T(8,128)(2,1)S(1)} %get-tuple-element.21), channel_id=3, replica_groups=mesh['ga'=2,'gx'=16,'gy'=8,'col'=2] {'col'}, dimensions={0}, use_global_device_ids=true | all-gather | bytes 1290240 | tf_op jit(solution)/shard_map/all_gather | solution.py:463
  111.5 1.5 triangle.1
  113.0 38.8 %all_to_all.10 = bf16[128,2,896]{2,1,0:T(2,128)(2,1)S(1)} all-to-all(bf16[128,2,896]{2,1,0:T(2,128)(2,1)S(1)} %triangle.1), channel_id=1, replica_groups=mesh['ga'=2,'gx'=16,'gy'=8,'col'=2] {'gy','gx'}, dimensions={0} | all-to-all | bytes 917504 | tf_op jit(solution)/shard_map/all_to_all | solution.py:473
  151.8 0.2 all_gather_reshape.3
  152.0 5.6 %all_gather.19.both_ref = bf16[2,256,896]{2,1,0:T(8,128)(2,1)S(1)} all-gather(bf16[1,256,896]{2,1,0:T(8,128)(2,1)S(1)} %all_gather_reshape.3), channel_id=1, replica_groups=mesh['ga'=2,'gx'=16,'gy'=8,'col'=2] {'col'}, dimensions={0}, use_global_device_ids=true | all-gather | bytes 1376256 | tf_op jit(solution)/shard_map/all_gather | solution.py:474
  157.7 2.4 %finish.1 = (bf16[40,64,80]{2,1,0:T(8,128)(2,1)}, f32[2,64]{1,0:T(2,128)}) custom-call(s32[1]{0:T(128)} %bitcast.half_ref, bf16[2,256,896]{2,1,0:T(8,128)(2,1)S(1)} %all_gather.19.both_ref, f32[2,128,896]{2,1,0:T(8,128)S(1)} %get-tuple-element.23.gating_ref, bf16[128,256]{1,0:T(8,128)(2,1)S(1)} %get-tuple-element.24.mixer_ref, ...), custom_call_target="tpu_custom_call" | custom-call | tf_op jit(solution)/shard_map/finish/pallas_call | solution.py:475
  (4 shorter events, 0.0 us)
Async XLA Ops:
  50.0 14.5 %copy-start.5 = (f32[128]{0:T(128)S(1)}, f32[128]{0:T(128)}, u32[]{:S(2)}) copy-start(f32[128]{0:T(128)} %param.18) | copy-start | bytes 1540
  50.0 14.5 %copy-start.6 = (f32[128]{0:T(128)S(1)}, f32[128]{0:T(128)}, u32[]{:S(2)}) copy-start(f32[128]{0:T(128)} %param.17) | copy-start | bytes 1540
  50.0 14.5 %copy-start.1 = (f32[128]{0:T(128)S(1)}, f32[128]{0:T(128)}, u32[]{:S(2)}) copy-start(f32[128]{0:T(128)} %param.13) | copy-start | bytes 1540
  50.0 14.5 %copy-start.2 = (f32[128]{0:T(128)S(1)}, f32[128]{0:T(128)}, u32[]{:S(2)}) copy-start(f32[128]{0:T(128)} %param.14) | copy-start | bytes 1540
  50.0 14.5 %copy-start.3 = (bf16[128,64]{0,1:T(8,128)(2,1)S(1)}, bf16[128,64]{0,1:T(8,128)(2,1)}, u32[]{:S(2)}) copy-start(bf16[128,64]{0,1:T(8,128)(2,1)} %param.16) | copy-start | bytes 49156
  50.0 14.5 %copy-start.4 = (bf16[128,64]{0,1:T(8,128)(2,1)S(1)}, bf16[128,64]{0,1:T(8,128)(2,1)}, u32[]{:S(2)}) copy-start(bf16[128,64]{0,1:T(8,128)(2,1)} %param.19) | copy-start | bytes 49156
  50.0 54.8 %all-to-all-start = ((bf16[128,2,1664]{2,1,0:T(2,128)(2,1)}), bf16[128,2,1664]{2,1,0:T(2,128)(2,1)S(1)}, u32[]{:S(2)}, u32[]{:S(2)}) async-start(bf16[128,2,1664]{2,1,0:T(2,128)(2,1)} %project.1), calls=%async_computation | async-start | bytes 1703936 | tf_op jit(solution)/shard_map/all_to_all | solution.py:432
  64.6 1.1 copy-start

commit v4 on v3

--- a/solution.py
+++ b/solution.py
@@ -152,11 +152,21 @@
     shift = span - (wide - LANES)
     inverse_ref[...] = format_limit / columns_of_parts(history_parts(packed_ref, outs), channels)
     even, odd = one_hot_rows(channels, 0), one_hot_rows(channels, 1)
-    for which in range(4):
-        here = pl.ds(which * outs, outs)
-        weight = jnp.concatenate([packed_ref[0, here, :], packed_ref[1, here, :]], axis=0)
-        weight = jnp.concatenate([nn(even, weight), nn(odd, weight)], axis=1).astype(BF16)
-        proj[which] = nt(weight, (near if which < 2 else far)[...])
+    weight = jnp.concatenate(
+        [
+            jnp.concatenate([packed_ref[0, at * outs : (at + 1) * outs], packed_ref[1, at * outs : (at + 1) * outs]], axis=0)
+            for at in range(4)
+        ],
+        axis=1,
+    )
+    evens, odds = nn(even, weight).astype(BF16), nn(odd, weight).astype(BF16)
+    for side in range(2):
+        both = [
+            jnp.concatenate([held[:, at * channels : (at + 1) * channels] for held in (evens, odds)], axis=1)
+            for at in (2 * side, 2 * side + 1)
+        ]
+        values = nt(jnp.concatenate(both, axis=0), (near if side == 0 else far)[...])
+        proj[2 * side : 2 * side + 2] = values.reshape(2, 2 * channels, wide)
     mask_near = jnp.concatenate([masks_ref[0]] * 2, axis=0)
     mask_far = jnp.concatenate([masks_ref[1]] * 2, axis=0)
     lane = lax.broadcasted_iota(jnp.int32, (16, LANES), 1)
@@ -195,7 +205,7 @@
         sent(at).wait()
         return carry
 
-    lax.fori_loop(0, channels // 8, step, 0)
+    lax.fori_loop(0, channels // 8, step, 0, unroll=8)
     lax.fori_loop(0, channels // 8, settle, 0)
 
 
@@ -318,7 +328,7 @@
 
 
 def finish_kernel(
-    half_ref, both_ref, gating_ref, mixer_ref, columns_ref, update_hbm, amax_ref, mixed, update_ref, sems, *, deep, cols
+    half_ref, both_ref, gating_ref, mixer_ref, columns_ref, update_ref, amax_ref, mixed, *, deep, cols
 ):
     rows, wide = both_ref.shape[1:]
     channels = rows // 2
@@ -326,10 +336,6 @@
     span = deep * cols
     gain, bias = columns_ref[:, 0:1], columns_ref[:, 1:2]
     mixer = mixer_ref[...]
-
-    def sent(at):
-        place = pl.ds(at * deep, deep)
-        return pltpu.make_async_copy(update_ref.at[place], update_hbm.at[place], sems.at[at])
 
     def per_part(values):
         total = jnp.sum(values, axis=0)
@@ -350,7 +356,6 @@
             for at in range(deep):
                 place = half * 2 * deep + part * deep + at
                 update_ref[place] = mixed[part * outs : (part + 1) * outs, at * cols : (at + 1) * cols]
-            sent(2 * half + part).start()
     last = both_ref[0, :, wide - LANES :]
     row = lax.broadcasted_iota(jnp.int32, (rows, outs), 0)
     col = lax.broadcasted_iota(jnp.int32, (rows, outs), 1)
@@ -359,8 +364,6 @@
     goal = span % LANES
     amax_ref[0:1, :] = sums[goal : goal + 1] + sums[goal + 1 : goal + 2] + sums[goal + 2 : goal + 3]
     amax_ref[1:2, :] = sums[goal + 3 : goal + 4] + sums[goal + 4 : goal + 5] + sums[goal + 5 : goal + 6]
-    for at in range(4):
-        sent(at).wait()
 
 
 VMEM = pl.BlockSpec(memory_space=pltpu.VMEM)
@@ -476,16 +479,12 @@
         functools.partial(finish_kernel, deep=deep, cols=cols),
         name="finish",
         out_shape=(
-            pltpu.HBM((rows, channels // 2, cols), BF16),
+            jax.ShapeDtypeStruct((rows, channels // 2, cols), BF16),
             jax.ShapeDtypeStruct((2, channels // 2), F32),
         ),
         in_specs=[SMEM] + [VMEM] * 4,
-        out_specs=(HBM, VMEM),
-        scratch_shapes=[
-            pltpu.VMEM((channels, wide), BF16),
-            pltpu.VMEM((rows, channels // 2, cols), BF16),
-            pltpu.SemaphoreType.DMA((4,)),
-        ],
+        out_specs=(VMEM,) * 2,
+        scratch_shapes=[pltpu.VMEM((channels, wide), BF16)],
         compiler_params=GRANT,
     )(half, both, gating, mixer, columns)
     return (jnp.transpose(update, (0, 2, 1))[None], new_amax)

time: 161 us -> 159 us (0.988)
  Pallas kernels: 14.1 us -> 12.2 us
where the time goes in v4:
time: 159 us; the launch traced here: 158 us
  blocking collectives  93.5 us (59%)
  waiting for transfers between devices  35.9 us (23%)
  starting transfers between devices  14.4 us (9%)
  Pallas kernels  12.2 us (8%)
    all_gather x1, blocking collectives, on_device(): packed = lax.all_gather(packed, 'col')  43 us
    all_to_all x1, blocking collectives, on_device(): lax.all_to_all(products, chips, split_axis=0, concat_axis=0, tiled=True)  38.8 us
    all_to_all x1, waiting for transfers between devices, on_device(): lax.all_to_all(message, chips, split_axis=0, concat_axis=0, tiled=True)  35.9 us
    all_to_all x1, starting transfers between devices, on_device(): lax.all_to_all(message, chips, split_axis=0, concat_axis=0, tiled=True)  14.4 us
    all_gather x1, blocking collectives, on_device(): both = lax.all_gather(right, 'col')  6.06 us
    all_gather x1, blocking collectives, on_device(): both = lax.all_gather(returned.reshape(2 * channels, -1), 'col')  5.63 us
    pallas_call x1, Pallas kernels, on_device(): pl.pallas_call(gate_kernel, name='gate', out_shape=(jax.ShapeDtypeStruct(...  3.19 us
  transfers between devices with their start and end apart: 1, of which 1 were waited for; matrix products, arithmetic and copies ran while one was open for 0% of the time, Pallas kernels for 2%

profile of v4, /device:TPU:65, one launch (start us, length us, event | category | flops | bytes accessed | tf_op | source)
XLA Modules:
  0.0 158.2 jit_solution(5056068106121764029)
XLA Ops:
  0.6 2.2 %prepare.1 = (bf16[272,128]{1,0:T(8,128)(2,1)S(1)}, bf16[896,256]{1,0:T(8,128)(2,1)S(1)}, bf16[896,256]{1,0:T(8,128)(2,1)S(1)}, f32[2,8,896]{2,1,0:T(8,128)S(1)}) custom-call(s32[1]{0:T(128)} %bitcast.half_ref, bf16[40,80,128]{2,1,0:T(8,128)(2,1)} %bitcast.17, s32[40,80]{1,0:T(8,128)} %bitcast.28, bf16[4,64,128]{2,1,0:T(8,128)(2,1)} %bitcast.27, ...), custom_call_target="tpu_custom_call" | custom-call | tf_op jit(solution)/shard_map/prepare/pallas_call | solution.py:398
  2.9 43.0 %all-gather = bf16[544,128]{1,0:T(8,128)(2,1)S(1)} all-gather(bf16[272,128]{1,0:T(8,128)(2,1)S(1)} %get-tuple-element.15), channel_id=2, replica_groups=mesh['ga'=2,'gx'=16,'gy'=8,'col'=2] {'col'}, dimensions={0}, use_global_device_ids=true | all-gather | bytes 208896 | tf_op jit(solution)/shard_map/all_gather | solution.py:420
  45.9 2.6 %project.1 = bf16[128,2,1664]{2,1,0:T(2,128)(2,1)} custom-call(bf16[2,272,128]{2,1,0:T(8,128)(2,1)S(1)} %bitcast.19, bf16[896,256]{1,0:T(8,128)(2,1)S(1)} %get-tuple-element.17.near, bf16[896,256]{1,0:T(8,128)(2,1)S(1)} %get-tuple-element.18.far, f32[2,8,896]{2,1,0:T(8,128)S(1)} %get-tuple-element.19.masks_ref), custom_call_target="tpu_custom_call" | custom-call | tf_op jit(solution)/shard_map/project/pallas_call | solution.py:421
  48.6 0.0 copy-start.5
  48.6 0.0 copy-start.6
  48.6 0.0 copy-start.1
  48.6 0.0 copy-start.2
  48.6 0.0 copy-start.3
  48.6 0.0 copy-start.4
  48.6 14.4 %all-to-all-start = ((bf16[128,2,1664]{2,1,0:T(2,128)(2,1)}), bf16[128,2,1664]{2,1,0:T(2,128)(2,1)S(1)}, u32[]{:S(2)}, u32[]{:S(2)}) async-start(bf16[128,2,1664]{2,1,0:T(2,128)(2,1)} %project.1), calls=%async_computation | async-start | bytes 1703936 | tf_op jit(solution)/shard_map/all_to_all | solution.py:435
  63.1 0.0 copy-done.5
  63.1 0.0 copy-done.6
  63.1 0.0 copy-done.1
  63.2 0.0 copy-start
  63.2 1.1 copy-done
  64.3 3.2 %gate.1 = (f32[2,128,896]{2,1,0:T(8,128)S(1)}, bf16[128,256]{1,0:T(8,128)(2,1)S(1)}, bf16[640,1024]{1,0:T(8,128)(2,1)S(1)}, f32[256,2]{1,0:T(8,128)S(1)}, f32[8,128]{1,0:T(8,128)S(1)}) custom-call(s32[1]{0:T(128)} %bitcast.1.mine_ref, bf16[40,80,128]{2,1,0:T(8,128)(2,1)S(1)} %bitcast.18, bf16[2,272,128]{2,1,0:T(8,128)(2,1)S(1)} %bitcast.20, ...), custom_call_target="tpu_custom_call" | custom-call | flops 20000000000 | bytes 3000000 | tf_op jit(solution)/shard_map/gate/pallas_call | solution.py:437
  67.5 35.9 %all-to-all-done.received_ref = bf16[128,2,1664]{2,1,0:T(2,128)(2,1)S(1)} async-done(((bf16[128,2,1664]{2,1,0:T(2,128)(2,1)}), bf16[128,2,1664]{2,1,0:T(2,128)(2,1)S(1)}, u32[]{:S(2)}, u32[]{:S(2)}) %all-to-all-start) | async-done | bytes 852000 | tf_op jit(solution)/shard_map/all_to_all | solution.py:435
  103.4 0.6 unpack.1
  104.0 6.1 %all-gather.1 = bf16[672,640]{1,0:T(8,128)(2,1)S(1)} all-gather(bf16[336,640]{1,0:T(8,128)(2,1)S(1)} %get-tuple-element.21), channel_id=3, replica_groups=mesh['ga'=2,'gx'=16,'gy'=8,'col'=2] {'col'}, dimensions={0}, use_global_device_ids=true | all-gather | bytes 1290240 | tf_op jit(solution)/shard_map/all_gather | solution.py:466
  110.1 1.5 triangle.1
  111.6 38.8 %all_to_all.10 = bf16[128,2,896]{2,1,0:T(2,128)(2,1)S(1)} all-to-all(bf16[128,2,896]{2,1,0:T(2,128)(2,1)S(1)} %triangle.1), channel_id=1, replica_groups=mesh['ga'=2,'gx'=16,'gy'=8,'col'=2] {'gy','gx'}, dimensions={0} | all-to-all | bytes 917504 | tf_op jit(solution)/shard_map/all_to_all | solution.py:476
  150.4 0.2 all_gather_reshape.3
  150.6 5.6 %all_gather.19.both_ref = bf16[2,256,896]{2,1,0:T(8,128)(2,1)S(1)} all-gather(bf16[1,256,896]{2,1,0:T(8,128)(2,1)S(1)} %all_gather_reshape.3), channel_id=1, replica_groups=mesh['ga'=2,'gx'=16,'gy'=8,'col'=2] {'col'}, dimensions={0}, use_global_device_ids=true | all-gather | bytes 1376256 | tf_op jit(solution)/shard_map/all_gather | solution.py:477
  156.2 2.0 %finish.1 = (bf16[40,64,80]{2,1,0:T(8,128)(2,1)}, f32[2,64]{1,0:T(2,128)}) custom-call(s32[1]{0:T(128)} %bitcast.half_ref, bf16[2,256,896]{2,1,0:T(8,128)(2,1)S(1)} %all_gather.19.both_ref, f32[2,128,896]{2,1,0:T(8,128)S(1)} %get-tuple-element.23.gating_ref, bf16[128,256]{1,0:T(8,128)(2,1)S(1)} %get-tuple-element.24.mixer_ref, ...), custom_call_target="tpu_custom_call" | custom-call | tf_op jit(solution)/shard_map/finish/pallas_call | solution.py:478
  (4 shorter events, 0.0 us)
Async XLA Ops:
  48.6 14.5 %copy-start.5 = (f32[128]{0:T(128)S(1)}, f32[128]{0:T(128)}, u32[]{:S(2)}) copy-start(f32[128]{0:T(128)} %param.18) | copy-start | bytes 1540
  48.6 14.5 %copy-start.6 = (f32[128]{0:T(128)S(1)}, f32[128]{0:T(128)}, u32[]{:S(2)}) copy-start(f32[128]{0:T(128)} %param.17) | copy-start | bytes 1540
  48.6 14.5 %copy-start.1 = (f32[128]{0:T(128)S(1)}, f32[128]{0:T(128)}, u32[]{:S(2)}) copy-start(f32[128]{0:T(128)} %param.13) | copy-start | bytes 1540
  48.6 14.5 %copy-start.2 = (f32[128]{0:T(128)S(1)}, f32[128]{0:T(128)}, u32[]{:S(2)}) copy-start(f32[128]{0:T(128)} %param.14) | copy-start | bytes 1540
  48.6 14.5 %copy-start.3 = (bf16[128,64]{0,1:T(8,128)(2,1)S(1)}, bf16[128,64]{0,1:T(8,128)(2,1)}, u32[]{:S(2)}) copy-start(bf16[128,64]{0,1:T(8,128)(2,1)} %param.16) | copy-start | bytes 49156
  48.6 14.5 %copy-start.4 = (bf16[128,64]{0,1:T(8,128)(2,1)S(1)}, bf16[128,64]{0,1:T(8,128)(2,1)}, u32[]{:S(2)}) copy-start(bf16[128,64]{0,1:T(8,128)(2,1)} %param.19) | copy-start | bytes 49156
  48.6 54.8 %all-to-all-start = ((bf16[128,2,1664]{2,1,0:T(2,128)(2,1)}), bf16[128,2,1664]{2,1,0:T(2,128)(2,1)S(1)}, u32[]{:S(2)}, u32[]{:S(2)}) async-start(bf16[128,2,1664]{2,1,0:T(2,128)(2,1)} %project.1), calls=%async_computation | async-start | bytes 1703936 | tf_op jit(solution)/shard_map/all_to_all | solution.py:435
  63.2 1.1 copy-start

commit v5 on v4

--- a/solution.py
+++ b/solution.py
@@ -123,11 +123,11 @@
     gain, bias = gain_ref[...], bias_ref[...]
     for part in range(2):
         copies[part].wait()
-        for at in range(deep):
-            block = normed_rows(rep_ref[part * deep + at].astype(F32), gain, bias)
-            lanes = slice(part * channels, (part + 1) * channels)
-            near[at * cols : (at + 1) * cols, lanes] = block
-            far[shift + at * cols : shift + (at + 1) * cols, lanes] = block
+        block = rep_ref[part * deep : (part + 1) * deep].reshape(span, channels)
+        block = normed_rows(block.astype(F32), gain, bias)
+        lanes = slice(part * channels, (part + 1) * channels)
+        near[0:span, lanes] = block
+        far[shift : shift + span, lanes] = block
     masks = mask_ref[...].astype(F32)
     masks = jnp.where(half == 0, masks[:held], masks[held:])
     pieces = [
@@ -238,11 +238,9 @@
     near[span:, :] = jnp.zeros((near.shape[0] - span, 2 * channels), BF16)
     for half in range(2):
         for part in range(2):
-            for at in range(deep):
-                block = rep_ref[half * (2 * deep) + part * deep + at].astype(F32)
-                near[at * cols : (at + 1) * cols, part * channels : (part + 1) * channels] = normed_rows(
-                    block, gain, bias
-                )
+            start = half * (2 * deep) + part * deep
+            block = rep_ref[start : start + deep].reshape(span, channels).astype(F32)
+            near[0:span, part * channels : (part + 1) * channels] = normed_rows(block, gain, bias)
         gating_ref[half] = jax.nn.sigmoid(nt(wide_gate, near[...]))
     columns_ref[...] = columns_of(affine_ref[...], channels)
     parts = history_parts(packed_ref, outs).astype(F32)
@@ -300,16 +298,14 @@
     block = count // deep
     span = deep * cols
     scale = scale_ref[0:1, 0:1]
-    total = None
     best = None
     for other in range(2):
-        products = nt(left_ref[...], both_ref[other, :count, :]) * scale
-        turned = nn(products.astype(BF16), order_ref[other * count : (other + 1) * count, :])
-        total = turned if total is None else total + turned
         parts = both_ref[other, count:, :LANES].astype(F32)
         parts = parts[0:1] + parts[1:2] + parts[2:3]
         best = parts if best is None else jnp.maximum(best, parts)
-    moved[...] = total.astype(BF16)
+    right = jnp.concatenate([both_ref[other, :count, :] for other in range(2)], axis=0)
+    products = nt(left_ref[...], right) * scale
+    moved[...] = nn(products.astype(BF16), order_ref[...]).astype(BF16)
     lane = lax.broadcasted_iota(jnp.int32, (8, LANES), 1)
     first = 2 * span % LANES
     goal = span % LANES

time: 159 us -> 158 us (level)
  Pallas kernels: 12.2 us -> 10 us
  transfers between devices with their start and end apart: 1 -> 1, of which waited for: 1 -> 1; matrix products, arithmetic and copies ran while one was open for 0% -> 0% of each run, Pallas kernels for 2% -> 1%
where the time goes in v5:
time: 158 us; the launch traced here: 157 us
  blocking collectives  93.5 us (59%)
  waiting for transfers between devices  37.3 us (24%)
  starting transfers between devices  14.4 us (9%)
  Pallas kernels  10 us (6%)
    all_gather x1, blocking collectives, on_device(): packed = lax.all_gather(packed, 'col')  43 us
    all_to_all x1, blocking collectives, on_device(): lax.all_to_all(products, chips, split_axis=0, concat_axis=0, tiled=True)  38.8 us
    all_to_all x1, waiting for transfers between devices, on_device(): lax.all_to_all(message, chips, split_axis=0, concat_axis=0, tiled=True)  37.3 us
    all_to_all x1, starting transfers between devices, on_device(): lax.all_to_all(message, chips, split_axis=0, concat_axis=0, tiled=True)  14.4 us
    all_gather x1, blocking collectives, on_device(): both = lax.all_gather(right, 'col')  6.06 us
    all_gather x1, blocking collectives, on_device(): both = lax.all_gather(returned.reshape(2 * channels, -1), 'col')  5.63 us
  transfers between devices with their start and end apart: 1, of which 1 were waited for; matrix products, arithmetic and copies ran while one was open for 0% of the time, Pallas kernels for 1%

profile of v5, /device:TPU:65, one launch (start us, length us, event | category | flops | bytes accessed | tf_op | source)
XLA Modules:
  0.0 157.5 jit_solution(12806450666175359267)
XLA Ops:
  0.6 1.8 %prepare.1 = (bf16[272,128]{1,0:T(8,128)(2,1)S(1)}, bf16[896,256]{1,0:T(8,128)(2,1)S(1)}, bf16[896,256]{1,0:T(8,128)(2,1)S(1)}, f32[2,8,896]{2,1,0:T(8,128)S(1)}) custom-call(s32[1]{0:T(128)} %bitcast.half_ref, bf16[40,80,128]{2,1,0:T(8,128)(2,1)} %bitcast.17, s32[40,80]{1,0:T(8,128)} %bitcast.28, bf16[4,64,128]{2,1,0:T(8,128)(2,1)} %bitcast.27, ...), custom_call_target="tpu_custom_call" | custom-call | tf_op jit(solution)/shard_map/prepare/pallas_call | solution.py:394
  2.4 43.0 %all-gather = bf16[544,128]{1,0:T(8,128)(2,1)S(1)} all-gather(bf16[272,128]{1,0:T(8,128)(2,1)S(1)} %get-tuple-element.15), channel_id=2, replica_groups=mesh['ga'=2,'gx'=16,'gy'=8,'col'=2] {'col'}, dimensions={0}, use_global_device_ids=true | all-gather | bytes 208896 | tf_op jit(solution)/shard_map/all_gather | solution.py:416
  45.5 2.6 %project.1 = bf16[128,2,1664]{2,1,0:T(2,128)(2,1)} custom-call(bf16[2,272,128]{2,1,0:T(8,128)(2,1)S(1)} %bitcast.19, bf16[896,256]{1,0:T(8,128)(2,1)S(1)} %get-tuple-element.17.near, bf16[896,256]{1,0:T(8,128)(2,1)S(1)} %get-tuple-element.18.far, f32[2,8,896]{2,1,0:T(8,128)S(1)} %get-tuple-element.19.masks_ref), custom_call_target="tpu_custom_call" | custom-call | tf_op jit(solution)/shard_map/project/pallas_call | solution.py:417
  48.1 0.0 copy-start.5
  48.1 0.0 copy-start.6
  48.1 0.0 copy-start.1
  48.2 0.0 copy-start.2
  48.2 0.0 copy-start.3
  48.2 0.0 copy-start.4
  48.2 14.4 %all-to-all-start = ((bf16[128,2,1664]{2,1,0:T(2,128)(2,1)}), bf16[128,2,1664]{2,1,0:T(2,128)(2,1)S(1)}, u32[]{:S(2)}, u32[]{:S(2)}) async-start(bf16[128,2,1664]{2,1,0:T(2,128)(2,1)} %project.1), calls=%async_computation | async-start | bytes 1703936 | tf_op jit(solution)/shard_map/all_to_all | solution.py:431
  62.7 0.0 copy-done.5
  62.7 0.0 copy-done.6
  62.7 0.0 copy-done.1
  62.7 0.0 copy-start
  62.7 1.1 copy-done
  63.9 1.8 %gate.1 = (f32[2,128,896]{2,1,0:T(8,128)S(1)}, bf16[128,256]{1,0:T(8,128)(2,1)S(1)}, bf16[640,1024]{1,0:T(8,128)(2,1)S(1)}, f32[256,2]{1,0:T(8,128)S(1)}, f32[8,128]{1,0:T(8,128)S(1)}) custom-call(s32[1]{0:T(128)} %bitcast.1.mine_ref, bf16[40,80,128]{2,1,0:T(8,128)(2,1)S(1)} %bitcast.18, bf16[2,272,128]{2,1,0:T(8,128)(2,1)S(1)} %bitcast.20, ...), custom_call_target="tpu_custom_call" | custom-call | flops 20000000000 | bytes 3000000 | tf_op jit(solution)/shard_map/gate/pallas_call | solution.py:433
  65.7 37.3 %all-to-all-done.received_ref = bf16[128,2,1664]{2,1,0:T(2,128)(2,1)S(1)} async-done(((bf16[128,2,1664]{2,1,0:T(2,128)(2,1)}), bf16[128,2,1664]{2,1,0:T(2,128)(2,1)S(1)}, u32[]{:S(2)}, u32[]{:S(2)}) %all-to-all-start) | async-done | bytes 852000 | tf_op jit(solution)/shard_map/all_to_all | solution.py:431
  103.0 0.6 unpack.1
  103.6 6.1 %all-gather.1 = bf16[672,640]{1,0:T(8,128)(2,1)S(1)} all-gather(bf16[336,640]{1,0:T(8,128)(2,1)S(1)} %get-tuple-element.21), channel_id=3, replica_groups=mesh['ga'=2,'gx'=16,'gy'=8,'col'=2] {'col'}, dimensions={0}, use_global_device_ids=true | all-gather | bytes 1290240 | tf_op jit(solution)/shard_map/all_gather | solution.py:462
  109.7 1.2 triangle.1
  110.9 38.8 %all_to_all.10 = bf16[128,2,896]{2,1,0:T(2,128)(2,1)S(1)} all-to-all(bf16[128,2,896]{2,1,0:T(2,128)(2,1)S(1)} %triangle.1), channel_id=1, replica_groups=mesh['ga'=2,'gx'=16,'gy'=8,'col'=2] {'gy','gx'}, dimensions={0} | all-to-all | bytes 917504 | tf_op jit(solution)/shard_map/all_to_all | solution.py:472
  149.7 0.2 all_gather_reshape.3
  149.9 5.6 %all_gather.19.both_ref = bf16[2,256,896]{2,1,0:T(8,128)(2,1)S(1)} all-gather(bf16[1,256,896]{2,1,0:T(8,128)(2,1)S(1)} %all_gather_reshape.3), channel_id=1, replica_groups=mesh['ga'=2,'gx'=16,'gy'=8,'col'=2] {'col'}, dimensions={0}, use_global_device_ids=true | all-gather | bytes 1376256 | tf_op jit(solution)/shard_map/all_gather | solution.py:473
  155.5 2.0 %finish.1 = (bf16[40,64,80]{2,1,0:T(8,128)(2,1)}, f32[2,64]{1,0:T(2,128)}) custom-call(s32[1]{0:T(128)} %bitcast.half_ref, bf16[2,256,896]{2,1,0:T(8,128)(2,1)S(1)} %all_gather.19.both_ref, f32[2,128,896]{2,1,0:T(8,128)S(1)} %get-tuple-element.23.gating_ref, bf16[128,256]{1,0:T(8,128)(2,1)S(1)} %get-tuple-element.24.mixer_ref, ...), custom_call_target="tpu_custom_call" | custom-call | tf_op jit(solution)/shard_map/finish/pallas_call | solution.py:474
  (4 shorter events, 0.0 us)
Async XLA Ops:
  48.1 14.5 %copy-start.5 = (f32[128]{0:T(128)S(1)}, f32[128]{0:T(128)}, u32[]{:S(2)}) copy-start(f32[128]{0:T(128)} %param.18) | copy-start | bytes 1540
  48.1 14.5 %copy-start.6 = (f32[128]{0:T(128)S(1)}, f32[128]{0:T(128)}, u32[]{:S(2)}) copy-start(f32[128]{0:T(128)} %param.17) | copy-start | bytes 1540
  48.1 14.5 %copy-start.1 = (f32[128]{0:T(128)S(1)}, f32[128]{0:T(128)}, u32[]{:S(2)}) copy-start(f32[128]{0:T(128)} %param.13) | copy-start | bytes 1540
  48.2 14.5 %copy-start.2 = (f32[128]{0:T(128)S(1)}, f32[128]{0:T(128)}, u32[]{:S(2)}) copy-start(f32[128]{0:T(128)} %param.14) | copy-start | bytes 1540
  48.2 14.5 %copy-start.3 = (bf16[128,64]{0,1:T(8,128)(2,1)S(1)}, bf16[128,64]{0,1:T(8,128)(2,1)}, u32[]{:S(2)}) copy-start(bf16[128,64]{0,1:T(8,128)(2,1)} %param.16) | copy-start | bytes 49156
  48.2 14.5 %copy-start.4 = (bf16[128,64]{0,1:T(8,128)(2,1)S(1)}, bf16[128,64]{0,1:T(8,128)(2,1)}, u32[]{:S(2)}) copy-start(bf16[128,64]{0,1:T(8,128)(2,1)} %param.19) | copy-start | bytes 49156
  48.2 54.8 %all-to-all-start = ((bf16[128,2,1664]{2,1,0:T(2,128)(2,1)}), bf16[128,2,1664]{2,1,0:T(2,128)(2,1)S(1)}, u32[]{:S(2)}, u32[]{:S(2)}) async-start(bf16[128,2,1664]{2,1,0:T(2,128)(2,1)} %project.1), calls=%async_computation | async-start | bytes 1703936 | tf_op jit(solution)/shard_map/all_to_all | solution.py:431
  62.7 1.1 copy-start

commit v6 on v5

--- a/solution.py
+++ b/solution.py
@@ -65,7 +65,7 @@
     return columns[:, 0:2] + columns[:, 2:4] + columns[:, 4:6]
 
 
-def prepare_kernel(
+def fetch_kernel(
     half_ref,
     rep_hbm,
     mask_hbm,
@@ -74,44 +74,31 @@
     gain_hbm,
     bias_hbm,
     packed_ref,
-    near,
-    far,
-    masks_ref,
     rep_ref,
     mask_ref,
+    affine_ref,
     weight_ref,
     history_ref,
-    gain_ref,
-    bias_ref,
     sems,
 ):
     which, outs, channels = weight_ref.shape
-    held, cols = rep_ref.shape[:2]
-    deep = held // 2
-    span = deep * cols
-    wide = near.shape[0]
-    shift = span - (wide - LANES)
-    half = half_ref[0]
+    held = rep_ref.shape[0]
     copies = [
         pltpu.make_async_copy(source, target, sems.at[at])
         for at, (source, target) in enumerate(
             (
-                (rep_hbm.at[pl.ds(half * held, deep)], rep_ref.at[pl.ds(0, deep)]),
-                (rep_hbm.at[pl.ds(half * held + deep, deep)], rep_ref.at[pl.ds(deep, deep)]),
-                (gain_hbm, gain_ref),
-                (bias_hbm, bias_ref),
-                (mask_hbm, mask_ref),
                 (weight_hbm, weight_ref),
                 (history_hbm, history_ref),
+                (rep_hbm.at[pl.ds(half_ref[0] * held, held)], rep_ref),
+                (gain_hbm, affine_ref.at[pl.ds(0, 1)]),
+                (bias_hbm, affine_ref.at[pl.ds(1, 1)]),
+                (mask_hbm, mask_ref),
             )
         )
     ]
     for copy in copies:
         copy.start()
-    near[pl.ds(span, wide - span), :] = jnp.zeros((wide - span, 2 * channels), BF16)
-    far[pl.ds(0, shift), :] = jnp.zeros((shift, 2 * channels), BF16)
-    far[pl.ds(shift + span, wide - span - shift), :] = jnp.zeros((wide - span - shift, 2 * channels), BF16)
-    for copy in copies[2:]:
+    for copy in copies[:2]:
         copy.wait()
     for at in range(which):
         packed_ref[at * outs : (at + 1) * outs, :] = weight_ref[at]
@@ -120,16 +107,28 @@
     parts = jnp.concatenate([parts, jnp.zeros_like(parts)], axis=1)
     parts = jnp.concatenate([parts, jnp.zeros_like(parts)], axis=0)
     packed_ref[which * outs :, :] = parts.astype(BF16)
-    gain, bias = gain_ref[...], bias_ref[...]
+    for copy in copies[2:]:
+        copy.wait()
+
+
+def norm_kernel(half_ref, rep_ref, mask_ref, affine_ref, near, far, masks_ref):
+    held, cols, channels = rep_ref.shape
+    deep = held // 2
+    span = deep * cols
+    wide = near.shape[0]
+    shift = span - (wide - LANES)
+    near[pl.ds(span, wide - span), :] = jnp.zeros((wide - span, 2 * channels), BF16)
+    far[pl.ds(0, shift), :] = jnp.zeros((shift, 2 * channels), BF16)
+    far[pl.ds(shift + span, wide - span - shift), :] = jnp.zeros((wide - span - shift, 2 * channels), BF16)
+    gain, bias = affine_ref[0:1, :], affine_ref[1:2, :]
     for part in range(2):
-        copies[part].wait()
         block = rep_ref[part * deep : (part + 1) * deep].reshape(span, channels)
         block = normed_rows(block.astype(F32), gain, bias)
         lanes = slice(part * channels, (part + 1) * channels)
         near[0:span, lanes] = block
         far[shift : shift + span, lanes] = block
     masks = mask_ref[...].astype(F32)
-    masks = jnp.where(half == 0, masks[:held], masks[held:])
+    masks = jnp.where(half_ref[0] == 0, masks[:held], masks[held:])
     pieces = [
         jnp.concatenate([masks[at : at + 1], masks[deep + at : deep + at + 1]], axis=0)
         for at in range(deep)
@@ -140,21 +139,26 @@
     masks_ref[1] = pltpu.roll(mask_near, shift, 1)
 
 
-def history_parts(packed_ref, outs):
-    start = packed_ref.shape[1] - 16
-    pieces = [packed_ref[col, start:, :][:, :outs] for col in range(2)]
-    return jnp.concatenate(pieces, axis=1)[:8]
-
-
-def project_kernel(packed_ref, near, far, masks_ref, out_hbm, proj, inverse_ref, out_ref, sems, *, span):
+def ordered(half, own_ref, other_ref):
+    own, other = own_ref[...].astype(F32), other_ref[...].astype(F32)
+    return [jnp.where(half == 0, own, other).astype(BF16), jnp.where(half == 0, other, own).astype(BF16)]
+
+
+def history_parts(packed, outs):
+    start = packed[0].shape[0] - 16
+    return jnp.concatenate([held[start:, :outs] for held in packed], axis=1)[:8]
+
+
+def project_kernel(half_ref, packed_ref, other_ref, near, far, masks_ref, out_hbm, proj, inverse_ref, out_ref, sems, *, span):
     wide, channels = near.shape[0], near.shape[1] // 2
     outs = channels // 2
     shift = span - (wide - LANES)
-    inverse_ref[...] = format_limit / columns_of_parts(history_parts(packed_ref, outs), channels)
+    packed = ordered(half_ref[0], packed_ref, other_ref)
+    inverse_ref[...] = format_limit / columns_of_parts(history_parts(packed, outs), channels)
     even, odd = one_hot_rows(channels, 0), one_hot_rows(channels, 1)
     weight = jnp.concatenate(
         [
-            jnp.concatenate([packed_ref[0, at * outs : (at + 1) * outs], packed_ref[1, at * outs : (at + 1) * outs]], axis=0)
+            jnp.concatenate([held[at * outs : (at + 1) * outs] for held in packed], axis=0)
             for at in range(4)
         ],
         axis=1,
@@ -210,9 +214,11 @@
 
 
 def gate_kernel(
+    half_ref,
     mine_ref,
     rep_ref,
     packed_ref,
+    other_ref,
     gate_ref,
     weight_ref,
     gain_ref,
@@ -243,7 +249,7 @@
             near[0:span, part * channels : (part + 1) * channels] = normed_rows(block, gain, bias)
         gating_ref[half] = jax.nn.sigmoid(nt(wide_gate, near[...]))
     columns_ref[...] = columns_of(affine_ref[...], channels)
-    parts = history_parts(packed_ref, outs).astype(F32)
+    parts = history_parts(ordered(half_ref[0], packed_ref, other_ref), outs).astype(F32)
     lane = lax.broadcasted_iota(jnp.int32, parts.shape, 1)
     parts = jnp.sum(jnp.where(lane == mine_ref[0], parts, 0.0), axis=1, keepdims=True)
     scales = (parts[0:2] + parts[2:4] + parts[4:6]) / format_limit
@@ -391,34 +397,43 @@
     rep = pair_rep[0]
     gain, bias = in_gain[None, :], in_bias[None, :]
 
-    packed, near, far, masks = pl.pallas_call(
-        prepare_kernel,
-        name="prepare",
+    packed, held, mask, affine = pl.pallas_call(
+        fetch_kernel,
+        name="fetch",
         out_shape=(
             jax.ShapeDtypeStruct((2 * channels + 16, channels), BF16),
+            jax.ShapeDtypeStruct((rows // 2, cols, channels), BF16),
+            jax.ShapeDtypeStruct((rows, cols), jnp.int32),
+            jax.ShapeDtypeStruct((2, channels), F32),
+        ),
+        in_specs=[SMEM] + [HBM] * 6,
+        out_specs=(VMEM,) * 4,
+        scratch_shapes=[
+            pltpu.VMEM((4, channels // 2, channels), BF16),
+            pltpu.VMEM((2, channels // 2), F32),
+            pltpu.SemaphoreType.DMA((6,)),
+        ],
+        compiler_params=GRANT,
+    )(half, *map(in_hbm, (rep, pair_mask[0], jnp.transpose(proj_weight, (1, 2, 0)), amax_history, gain, bias)))
+    other = lax.ppermute(packed, "col", [(0, 1), (1, 0)])
+    near, far, masks = pl.pallas_call(
+        norm_kernel,
+        name="norm",
+        out_shape=(
             jax.ShapeDtypeStruct((wide, 2 * channels), BF16),
             jax.ShapeDtypeStruct((wide, 2 * channels), BF16),
             jax.ShapeDtypeStruct((2, 8, wide), F32),
         ),
-        in_specs=[SMEM] + [HBM] * 6,
-        out_specs=(VMEM,) * 4,
-        scratch_shapes=[
-            pltpu.VMEM((rows // 2, cols, channels), BF16),
-            pltpu.VMEM((rows, cols), jnp.int32),
-            pltpu.VMEM((4, channels // 2, channels), BF16),
-            pltpu.VMEM((2, channels // 2), F32),
-            pltpu.VMEM((1, channels), F32),
-            pltpu.VMEM((1, channels), F32),
-            pltpu.SemaphoreType.DMA((7,)),
-        ],
-        compiler_params=GRANT,
-    )(half, *map(in_hbm, (rep, pair_mask[0], jnp.transpose(proj_weight, (1, 2, 0)), amax_history, gain, bias)))
-    packed = lax.all_gather(packed, "col")
+        in_specs=[SMEM] + [VMEM] * 3,
+        out_specs=(VMEM,) * 3,
+        compiler_params=GRANT,
+        cost_estimate=pl.CostEstimate(flops=20_000_000_000, bytes_accessed=3_000_000, transcendentals=0),
+    )(half, held, mask, affine)
     message = pl.pallas_call(
         functools.partial(project_kernel, span=span),
         name="project",
         out_shape=pltpu.HBM((channels, 2, 2 * wide - LANES), BF16),
-        in_specs=[VMEM] * 4,
+        in_specs=[SMEM] + [VMEM] * 5,
         out_specs=HBM,
         scratch_shapes=[
             pltpu.VMEM((4, 2 * channels, wide), F32),
@@ -427,7 +442,7 @@
             pltpu.SemaphoreType.DMA((channels // 8,)),
         ],
         compiler_params=GRANT,
-    )(packed, near, far, masks)
+    )(half, packed, other, near, far, masks)
     received = lax.all_to_all(message, chips, split_axis=0, concat_axis=0, tiled=True)
     mine = lax.axis_index(chips).reshape(1).astype(jnp.int32)
     gating, mixer, order, columns, scale = pl.pallas_call(
@@ -440,12 +455,12 @@
             jax.ShapeDtypeStruct((2 * channels, 2), F32),
             jax.ShapeDtypeStruct((8, LANES), F32),
         ),
-        in_specs=[SMEM] + [VMEM] * 7,
+        in_specs=[SMEM] * 2 + [VMEM] * 8,
         out_specs=(VMEM,) * 5,
         scratch_shapes=[pltpu.VMEM((wide, 2 * channels), BF16)],
         compiler_params=GRANT,
         cost_estimate=pl.CostEstimate(flops=20_000_000_000, bytes_accessed=3_000_000, transcendentals=0),
-    )(mine, rep, packed, gate_weight.T, out_weight.T, gain, bias, jnp.stack([out_gain, out_bias]))
+    )(half, mine, rep, packed, other, gate_weight.T, out_weight.T, gain, bias, jnp.stack([out_gain, out_bias]))
     count = ranks * rows // 2
     left, right = pl.pallas_call(
         functools.partial(unpack_kernel, groups=groups, deep=deep, cols=cols),

time: 158 us -> 158 us (level)
  starting transfers between devices: 14.4 us -> 57.8 us
  blocking collectives: 93.5 us -> 50.5 us
    ppermute x0 -> x1, starting transfers between devices: none -> 43.4 us  [on_device(): other = lax.ppermute(packed, 'col', [(0, 1), (1, 0)])]
    all_gather x1 -> x0, blocking collectives: 43 us -> none  [on_device(): packed = lax.all_gather(packed, 'col')]
  transfers between devices with their start and end apart: 1 -> 2, of which waited for: 1 -> 2; matrix products, arithmetic and copies ran while one was open for 0% -> 0% of each run, Pallas kernels for 1% -> 1%
where the time goes in v6:
time: 158 us
  starting transfers between devices  57.8 us (37%)
  blocking collectives  50.5 us (32%)
  waiting for transfers between devices  37.6 us (24%)
  Pallas kernels  9.91 us (6%)
    ppermute x1, starting transfers between devices, on_device(): other = lax.ppermute(packed, 'col', [(0, 1), (1, 0)])  43.4 us
    all_to_all x1, blocking collectives, on_device(): lax.all_to_all(products, chips, split_axis=0, concat_axis=0, tiled=True)  38.8 us
    all_to_all x1, waiting for transfers between devices, on_device(): lax.all_to_all(message, chips, split_axis=0, concat_axis=0, tiled=True)  37.3 us
    all_to_all x1, starting transfers between devices, on_device(): lax.all_to_all(message, chips, split_axis=0, concat_axis=0, tiled=True)  14.4 us
    all_gather x1, blocking collectives, on_device(): both = lax.all_gather(right, 'col')  6.06 us
    all_gather x1, blocking collectives, on_device(): both = lax.all_gather(returned.reshape(2 * channels, -1), 'col')  5.63 us
  transfers between devices with their start and end apart: 2, of which 2 were waited for; matrix products, arithmetic and copies ran while one was open for 0% of the time, Pallas kernels for 1%

profile of v6, /device:TPU:65, one launch (start us, length us, event | category | flops | bytes accessed | tf_op | source)
XLA Modules:
  0.0 158.0 jit_solution(8927960852913450284)
XLA Ops:
  0.6 1.1 fetch.1
  1.8 43.4 %collective-permute-start = (bf16[272,128]{1,0:T(8,128)(2,1)S(1)}, bf16[272,128]{1,0:T(8,128)(2,1)S(1)}, u32[]{:S(2)}, u32[]{:S(2)}) collective-permute-start(bf16[272,128]{1,0:T(8,128)(2,1)S(1)} %get-tuple-element.18.packed_ref), channel_id=1, source_target_pairs={{0,1},{1,0},{2,3},{3,2},{4,5},{5,4},{6,7},{7,6},{8,9},{9,8},{10,11... | collective-permute-start | bytes 208904 | tf_op jit(solution)/shard_map/ppermute | solution.py:418
  45.1 0.6 norm.1
  45.7 0.3 collective-permute-done.other_ref
  46.0 2.7 %project.1 = bf16[128,2,1664]{2,1,0:T(2,128)(2,1)} custom-call(s32[1]{0:T(128)} %bitcast.half_ref, bf16[272,128]{1,0:T(8,128)(2,1)S(1)} %get-tuple-element.18.packed_ref, bf16[272,128]{1,0:T(8,128)(2,1)S(1)} %collective-permute-done.other_ref, bf16[896,256]{1,0:T(8,128)(2,1)S(1)} %get-tuple-element.23.near, bf16[896,256]{1,0:T(8,128)(2,1)S(1)} %get-tuple-element.24.far, ...), custom_call_target="tpu_custom_call" | custom-call | tf_op jit(solution)/shard_map/project/pallas_call | solution.py:432
  48.7 0.0 copy-start.5
  48.7 0.0 copy-start.6
  48.7 0.0 copy-start.1
  48.7 0.0 copy-start.2
  48.7 0.0 copy-start.3
  48.7 0.0 copy-start.4
  48.8 14.4 %all-to-all-start = ((bf16[128,2,1664]{2,1,0:T(2,128)(2,1)}), bf16[128,2,1664]{2,1,0:T(2,128)(2,1)S(1)}, u32[]{:S(2)}, u32[]{:S(2)}) async-start(bf16[128,2,1664]{2,1,0:T(2,128)(2,1)} %project.1), calls=%async_computation | async-start | bytes 1703936 | tf_op jit(solution)/shard_map/all_to_all | solution.py:446
  63.2 0.0 copy-done.5
  63.3 0.0 copy-start
  63.3 1.1 copy-done
  64.4 1.8 %gate.1 = (f32[2,128,896]{2,1,0:T(8,128)S(1)}, bf16[128,256]{1,0:T(8,128)(2,1)S(1)}, bf16[640,1024]{1,0:T(8,128)(2,1)S(1)}, f32[256,2]{1,0:T(8,128)S(1)}, f32[8,128]{1,0:T(8,128)S(1)}) custom-call(s32[1]{0:T(128)} %bitcast.half_ref, s32[1]{0:T(128)} %bitcast.1.mine_ref, bf16[40,80,128]{2,1,0:T(8,128)(2,1)S(1)} %bitcast.17, ...), custom_call_target="tpu_custom_call" | custom-call | flops 20000000000 | bytes 3000000 | tf_op jit(solution)/shard_map/gate/pallas_call | solution.py:448
  66.2 37.3 %all-to-all-done.received_ref = bf16[128,2,1664]{2,1,0:T(2,128)(2,1)S(1)} async-done(((bf16[128,2,1664]{2,1,0:T(2,128)(2,1)}), bf16[128,2,1664]{2,1,0:T(2,128)(2,1)S(1)}, u32[]{:S(2)}, u32[]{:S(2)}) %all-to-all-start) | async-done | bytes 852000 | tf_op jit(solution)/shard_map/all_to_all | solution.py:446
  103.5 0.6 unpack.1
  104.2 6.1 %all-gather = bf16[672,640]{1,0:T(8,128)(2,1)S(1)} all-gather(bf16[336,640]{1,0:T(8,128)(2,1)S(1)} %get-tuple-element.27), channel_id=2, replica_groups=mesh['ga'=2,'gx'=16,'gy'=8,'col'=2] {'col'}, dimensions={0}, use_global_device_ids=true | all-gather | bytes 1290240 | tf_op jit(solution)/shard_map/all_gather | solution.py:477
  110.2 1.2 triangle.1
  111.4 38.8 %all_to_all.10 = bf16[128,2,896]{2,1,0:T(2,128)(2,1)S(1)} all-to-all(bf16[128,2,896]{2,1,0:T(2,128)(2,1)S(1)} %triangle.1), channel_id=1, replica_groups=mesh['ga'=2,'gx'=16,'gy'=8,'col'=2] {'gy','gx'}, dimensions={0} | all-to-all | bytes 917504 | tf_op jit(solution)/shard_map/all_to_all | solution.py:487
  150.3 0.2 all_gather_reshape.3
  150.4 5.6 %all_gather.11.both_ref = bf16[2,256,896]{2,1,0:T(8,128)(2,1)S(1)} all-gather(bf16[1,256,896]{2,1,0:T(8,128)(2,1)S(1)} %all_gather_reshape.3), channel_id=1, replica_groups=mesh['ga'=2,'gx'=16,'gy'=8,'col'=2] {'col'}, dimensions={0}, use_global_device_ids=true | all-gather | bytes 1376256 | tf_op jit(solution)/shard_map/all_gather | solution.py:488
  156.1 2.0 %finish.1 = (bf16[40,64,80]{2,1,0:T(8,128)(2,1)}, f32[2,64]{1,0:T(2,128)}) custom-call(s32[1]{0:T(128)} %bitcast.half_ref, bf16[2,256,896]{2,1,0:T(8,128)(2,1)S(1)} %all_gather.11.both_ref, f32[2,128,896]{2,1,0:T(8,128)S(1)} %get-tuple-element.29.gating_ref, bf16[128,256]{1,0:T(8,128)(2,1)S(1)} %get-tuple-element.30.mixer_ref, ...), custom_call_target="tpu_custom_call" | custom-call | tf_op jit(solution)/shard_map/finish/pallas_call | solution.py:489
  (6 shorter events, 0.0 us)
Async XLA Ops:
  1.8 44.3 %collective-permute-start = (bf16[272,128]{1,0:T(8,128)(2,1)S(1)}, bf16[272,128]{1,0:T(8,128)(2,1)S(1)}, u32[]{:S(2)}, u32[]{:S(2)}) collective-permute-start(bf16[272,128]{1,0:T(8,128)(2,1)S(1)} %get-tuple-element.18.packed_ref), channel_id=1, source_target_pairs={{0,1},{1,0},{2,3},{3,2},{4,5},{5,4},{6,7},{7,6},{8,9},{9,8},{10,11... | collective-permute-start | bytes 208904 | tf_op jit(solution)/shard_map/ppermute | solution.py:418
  48.7 14.5 %copy-start.5 = (f32[128]{0:T(128)S(1)}, f32[128]{0:T(128)}, u32[]{:S(2)}) copy-start(f32[128]{0:T(128)} %param.18) | copy-start | bytes 1540
  48.7 14.5 %copy-start.6 = (f32[128]{0:T(128)S(1)}, f32[128]{0:T(128)}, u32[]{:S(2)}) copy-start(f32[128]{0:T(128)} %param.17) | copy-start | bytes 1540
  48.7 14.5 %copy-start.1 = (f32[128]{0:T(128)S(1)}, f32[128]{0:T(128)}, u32[]{:S(2)}) copy-start(f32[128]{0:T(128)} %param.13) | copy-start | bytes 1540
  48.7 14.5 %copy-start.2 = (f32[128]{0:T(128)S(1)}, f32[128]{0:T(128)}, u32[]{:S(2)}) copy-start(f32[128]{0:T(128)} %param.14) | copy-start | bytes 1540
  48.7 14.5 %copy-start.3 = (bf16[128,64]{0,1:T(8,128)(2,1)S(1)}, bf16[128,64]{0,1:T(8,128)(2,1)}, u32[]{:S(2)}) copy-start(bf16[128,64]{0,1:T(8,128)(2,1)} %param.16) | copy-start | bytes 49156
  48.7 14.5 %copy-start.4 = (bf16[128,64]{0,1:T(8,128)(2,1)S(1)}, bf16[128,64]{0,1:T(8,128)(2,1)}, u32[]{:S(2)}) copy-start(bf16[128,64]{0,1:T(8,128)(2,1)} %param.19) | copy-start | bytes 49156
  48.8 54.8 %all-to-all-start = ((bf16[128,2,1664]{2,1,0:T(2,128)(2,1)}), bf16[128,2,1664]{2,1,0:T(2,128)(2,1)S(1)}, u32[]{:S(2)}, u32[]{:S(2)}) async-start(bf16[128,2,1664]{2,1,0:T(2,128)(2,1)} %project.1), calls=%async_computation | async-start | bytes 1703936 | tf_op jit(solution)/shard_map/all_to_all | solution.py:446
  63.3 1.1 copy-start

commit v7 on v6

--- a/solution.py
+++ b/solution.py
@@ -111,7 +111,15 @@
         copy.wait()
 
 
-def norm_kernel(half_ref, rep_ref, mask_ref, affine_ref, near, far, masks_ref):
+def history_parts(packed_ref, outs):
+    start = packed_ref.shape[1] - 16
+    pieces = [packed_ref[col, start:, :][:, :outs] for col in range(2)]
+    return jnp.concatenate(pieces, axis=1)[:8]
+
+
+def project_kernel(
+    half_ref, packed_ref, rep_ref, mask_ref, affine_ref, out_hbm, near, far, proj, inverse_ref, out_ref, sems
+):
     held, cols, channels = rep_ref.shape
     deep = held // 2
     span = deep * cols
@@ -135,30 +143,14 @@
     ]
     zeros = jnp.zeros((2, wide - span), F32)
     mask_near = jnp.concatenate([jnp.concatenate([*pieces, zeros], axis=1)] * 4, axis=0)
-    masks_ref[0] = mask_near
-    masks_ref[1] = pltpu.roll(mask_near, shift, 1)
-
-
-def ordered(half, own_ref, other_ref):
-    own, other = own_ref[...].astype(F32), other_ref[...].astype(F32)
-    return [jnp.where(half == 0, own, other).astype(BF16), jnp.where(half == 0, other, own).astype(BF16)]
-
-
-def history_parts(packed, outs):
-    start = packed[0].shape[0] - 16
-    return jnp.concatenate([held[start:, :outs] for held in packed], axis=1)[:8]
-
-
-def project_kernel(half_ref, packed_ref, other_ref, near, far, masks_ref, out_hbm, proj, inverse_ref, out_ref, sems, *, span):
-    wide, channels = near.shape[0], near.shape[1] // 2
+    mask_far = jnp.concatenate([pltpu.roll(mask_near, shift, 1)] * 2, axis=0)
+    mask_near = jnp.concatenate([mask_near] * 2, axis=0)
     outs = channels // 2
-    shift = span - (wide - LANES)
-    packed = ordered(half_ref[0], packed_ref, other_ref)
-    inverse_ref[...] = format_limit / columns_of_parts(history_parts(packed, outs), channels)
+    inverse_ref[...] = format_limit / columns_of_parts(history_parts(packed_ref, outs), channels)
     even, odd = one_hot_rows(channels, 0), one_hot_rows(channels, 1)
     weight = jnp.concatenate(
         [
-            jnp.concatenate([held[at * outs : (at + 1) * outs] for held in packed], axis=0)
+            jnp.concatenate([packed_ref[0, at * outs : (at + 1) * outs], packed_ref[1, at * outs : (at + 1) * outs]], axis=0)
             for at in range(4)
         ],
         axis=1,
@@ -171,8 +163,6 @@
         ]
         values = nt(jnp.concatenate(both, axis=0), (near if side == 0 else far)[...])
         proj[2 * side : 2 * side + 2] = values.reshape(2, 2 * channels, wide)
-    mask_near = jnp.concatenate([masks_ref[0]] * 2, axis=0)
-    mask_far = jnp.concatenate([masks_ref[1]] * 2, axis=0)
     lane = lax.broadcasted_iota(jnp.int32, (16, LANES), 1)
     first = shift + span - (wide - LANES)
 
@@ -214,11 +204,9 @@
 
 
 def gate_kernel(
-    half_ref,
     mine_ref,
     rep_ref,
     packed_ref,
-    other_ref,
     gate_ref,
     weight_ref,
     gain_ref,
@@ -249,7 +237,7 @@
             near[0:span, part * channels : (part + 1) * channels] = normed_rows(block, gain, bias)
         gating_ref[half] = jax.nn.sigmoid(nt(wide_gate, near[...]))
     columns_ref[...] = columns_of(affine_ref[...], channels)
-    parts = history_parts(ordered(half_ref[0], packed_ref, other_ref), outs).astype(F32)
+    parts = history_parts(packed_ref, outs).astype(F32)
     lane = lax.broadcasted_iota(jnp.int32, parts.shape, 1)
     parts = jnp.sum(jnp.where(lane == mine_ref[0], parts, 0.0), axis=1, keepdims=True)
     scales = (parts[0:2] + parts[2:4] + parts[4:6]) / format_limit
@@ -415,34 +403,23 @@
         ],
         compiler_params=GRANT,
     )(half, *map(in_hbm, (rep, pair_mask[0], jnp.transpose(proj_weight, (1, 2, 0)), amax_history, gain, bias)))
-    other = lax.ppermute(packed, "col", [(0, 1), (1, 0)])
-    near, far, masks = pl.pallas_call(
-        norm_kernel,
-        name="norm",
-        out_shape=(
-            jax.ShapeDtypeStruct((wide, 2 * channels), BF16),
-            jax.ShapeDtypeStruct((wide, 2 * channels), BF16),
-            jax.ShapeDtypeStruct((2, 8, wide), F32),
-        ),
-        in_specs=[SMEM] + [VMEM] * 3,
-        out_specs=(VMEM,) * 3,
-        compiler_params=GRANT,
-        cost_estimate=pl.CostEstimate(flops=20_000_000_000, bytes_accessed=3_000_000, transcendentals=0),
-    )(half, held, mask, affine)
+    packed = lax.all_gather(packed, "col")
     message = pl.pallas_call(
-        functools.partial(project_kernel, span=span),
+        project_kernel,
         name="project",
         out_shape=pltpu.HBM((channels, 2, 2 * wide - LANES), BF16),
-        in_specs=[SMEM] + [VMEM] * 5,
+        in_specs=[SMEM] + [VMEM] * 4,
         out_specs=HBM,
         scratch_shapes=[
+            pltpu.VMEM((wide, 2 * channels), BF16),
+            pltpu.VMEM((wide, 2 * channels), BF16),
             pltpu.VMEM((4, 2 * channels, wide), F32),
             pltpu.VMEM((2 * channels, 2), F32),
             pltpu.VMEM((channels, 2, 2 * wide - LANES), BF16),
             pltpu.SemaphoreType.DMA((channels // 8,)),
         ],
         compiler_params=GRANT,
-    )(half, packed, other, near, far, masks)
+    )(half, packed, held, mask, affine)
     received = lax.all_to_all(message, chips, split_axis=0, concat_axis=0, tiled=True)
     mine = lax.axis_index(chips).reshape(1).astype(jnp.int32)
     gating, mixer, order, columns, scale = pl.pallas_call(
@@ -455,12 +432,12 @@
             jax.ShapeDtypeStruct((2 * channels, 2), F32),
             jax.ShapeDtypeStruct((8, LANES), F32),
         ),
-        in_specs=[SMEM] * 2 + [VMEM] * 8,
+        in_specs=[SMEM] + [VMEM] * 7,
         out_specs=(VMEM,) * 5,
         scratch_shapes=[pltpu.VMEM((wide, 2 * channels), BF16)],
         compiler_params=GRANT,
         cost_estimate=pl.CostEstimate(flops=20_000_000_000, bytes_accessed=3_000_000, transcendentals=0),
-    )(half, mine, rep, packed, other, gate_weight.T, out_weight.T, gain, bias, jnp.stack([out_gain, out_bias]))
+    )(mine, rep, packed, gate_weight.T, out_weight.T, gain, bias, jnp.stack([out_gain, out_bias]))
     count = ranks * rows // 2
     left, right = pl.pallas_call(
         functools.partial(unpack_kernel, groups=groups, deep=deep, cols=cols),

time: 158 us -> 157 us (level)
  starting transfers between devices: 57.8 us -> 14.3 us
  blocking collectives: 50.5 us -> 93.5 us
    ppermute x1 -> x0, starting transfers between devices: 43.4 us -> none  [on_device(): other = lax.ppermute(packed, 'col', [(0, 1), (1, 0)])]
    all_gather x0 -> x1, blocking collectives: none -> 43 us  [on_device(): packed = lax.all_gather(packed, 'col')]
    pallas_call x2 -> x1, Pallas kernels: 3.2 us -> 2.93 us  [on_device(): pl.pallas_call(project_kernel, name='project', out_shape=pltpu.HBM((chann...]
  transfers between devices with their start and end apart: 2 -> 1, of which waited for: 2 -> 1; matrix products, arithmetic and copies ran while one was open for 0% -> 0% of each run, Pallas kernels for 1% -> 1%
where the time goes in v7:
time: 157 us
  blocking collectives  93.5 us (60%)
  waiting for transfers between devices  37.3 us (24%)
  starting transfers between devices  14.3 us (9%)
  Pallas kernels  9.62 us (6%)
    all_gather x1, blocking collectives, on_device(): packed = lax.all_gather(packed, 'col')  43 us
    all_to_all x1, blocking collectives, on_device(): lax.all_to_all(products, chips, split_axis=0, concat_axis=0, tiled=True)  38.8 us
    all_to_all x1, waiting for transfers between devices, on_device(): lax.all_to_all(message, chips, split_axis=0, concat_axis=0, tiled=True)  37.3 us
    all_to_all x1, starting transfers between devices, on_device(): lax.all_to_all(message, chips, split_axis=0, concat_axis=0, tiled=True)  14.3 us
    all_gather x1, blocking collectives, on_device(): both = lax.all_gather(right, 'col')  6.06 us
    all_gather x1, blocking collectives, on_device(): both = lax.all_gather(returned.reshape(2 * channels, -1), 'col')  5.63 us
  transfers between devices with their start and end apart: 1, of which 1 were waited for; matrix products, arithmetic and copies ran while one was open for 0% of the time, Pallas kernels for 1%

profile of v7, /device:TPU:65, one launch (start us, length us, event | category | flops | bytes accessed | tf_op | source)
XLA Modules:
  0.0 156.9 jit_solution(10836189781458197825)
XLA Ops:
  0.6 1.1 fetch.1
  1.8 43.0 %all-gather = bf16[544,128]{1,0:T(8,128)(2,1)S(1)} all-gather(bf16[272,128]{1,0:T(8,128)(2,1)S(1)} %get-tuple-element.15), channel_id=2, replica_groups=mesh['ga'=2,'gx'=16,'gy'=8,'col'=2] {'col'}, dimensions={0}, use_global_device_ids=true | all-gather | bytes 208896 | tf_op jit(solution)/shard_map/all_gather | solution.py:406
  44.8 0.0 copy-start.5
  44.8 0.0 copy-start.1
  44.8 0.0 copy-start.4
  44.8 2.9 %project.1 = bf16[128,2,1664]{2,1,0:T(2,128)(2,1)} custom-call(s32[1]{0:T(128)} %bitcast.half_ref, bf16[2,272,128]{2,1,0:T(8,128)(2,1)S(1)} %bitcast.19, bf16[20,80,128]{2,1,0:T(8,128)(2,1)S(1)} %get-tuple-element.17.rep_ref, s32[40,80]{1,0:T(8,128)S(1)} %get-tuple-element.18.mask_ref, f32[2,128]{1,0:T(2,128)S(1)} %get-tuple-element.19.affine_ref), custom_call_target="tpu_custom_call" | custom-call | tf_op jit(solution)/shard_map/project/pallas_call | solution.py:407
  47.8 14.3 %all-to-all-start = ((bf16[128,2,1664]{2,1,0:T(2,128)(2,1)}), bf16[128,2,1664]{2,1,0:T(2,128)(2,1)S(1)}, u32[]{:S(2)}, u32[]{:S(2)}) async-start(bf16[128,2,1664]{2,1,0:T(2,128)(2,1)} %project.1), calls=%async_computation | async-start | bytes 1703936 | tf_op jit(solution)/shard_map/all_to_all | solution.py:423
  62.1 0.0 copy-done.5
  62.1 0.0 copy-done.6
  62.1 0.0 copy-done.1
  62.1 0.0 copy-done.2
  62.1 0.0 copy-done.3
  62.2 0.0 copy-done.4
  62.2 0.0 copy-start
  62.2 1.1 copy-done
  63.3 1.8 %gate.1 = (f32[2,128,896]{2,1,0:T(8,128)S(1)}, bf16[128,256]{1,0:T(8,128)(2,1)S(1)}, bf16[640,1024]{1,0:T(8,128)(2,1)S(1)}, f32[256,2]{1,0:T(8,128)S(1)}, f32[8,128]{1,0:T(8,128)S(1)}) custom-call(s32[1]{0:T(128)} %bitcast.1.mine_ref, bf16[40,80,128]{2,1,0:T(8,128)(2,1)S(1)} %bitcast.18, bf16[2,272,128]{2,1,0:T(8,128)(2,1)S(1)} %bitcast.20, ...), custom_call_target="tpu_custom_call" | custom-call | flops 20000000000 | bytes 3000000 | tf_op jit(solution)/shard_map/gate/pallas_call | solution.py:425
  65.1 37.3 %all-to-all-done.received_ref = bf16[128,2,1664]{2,1,0:T(2,128)(2,1)S(1)} async-done(((bf16[128,2,1664]{2,1,0:T(2,128)(2,1)}), bf16[128,2,1664]{2,1,0:T(2,128)(2,1)S(1)}, u32[]{:S(2)}, u32[]{:S(2)}) %all-to-all-start) | async-done | bytes 852000 | tf_op jit(solution)/shard_map/all_to_all | solution.py:423
  102.4 0.6 unpack.1
  103.0 6.1 %all-gather.1 = bf16[672,640]{1,0:T(8,128)(2,1)S(1)} all-gather(bf16[336,640]{1,0:T(8,128)(2,1)S(1)} %get-tuple-element.21), channel_id=3, replica_groups=mesh['ga'=2,'gx'=16,'gy'=8,'col'=2] {'col'}, dimensions={0}, use_global_device_ids=true | all-gather | bytes 1290240 | tf_op jit(solution)/shard_map/all_gather | solution.py:454
  109.1 1.2 triangle.1
  110.3 38.8 %all_to_all.10 = bf16[128,2,896]{2,1,0:T(2,128)(2,1)S(1)} all-to-all(bf16[128,2,896]{2,1,0:T(2,128)(2,1)S(1)} %triangle.1), channel_id=1, replica_groups=mesh['ga'=2,'gx'=16,'gy'=8,'col'=2] {'gy','gx'}, dimensions={0} | all-to-all | bytes 917504 | tf_op jit(solution)/shard_map/all_to_all | solution.py:464
  149.1 0.2 all_gather_reshape.3
  149.3 5.6 %all_gather.19.both_ref = bf16[2,256,896]{2,1,0:T(8,128)(2,1)S(1)} all-gather(bf16[1,256,896]{2,1,0:T(8,128)(2,1)S(1)} %all_gather_reshape.3), channel_id=1, replica_groups=mesh['ga'=2,'gx'=16,'gy'=8,'col'=2] {'col'}, dimensions={0}, use_global_device_ids=true | all-gather | bytes 1376256 | tf_op jit(solution)/shard_map/all_gather | solution.py:465
  154.9 2.0 %finish.1 = (bf16[40,64,80]{2,1,0:T(8,128)(2,1)}, f32[2,64]{1,0:T(2,128)}) custom-call(s32[1]{0:T(128)} %bitcast.half_ref, bf16[2,256,896]{2,1,0:T(8,128)(2,1)S(1)} %all_gather.19.both_ref, f32[2,128,896]{2,1,0:T(8,128)S(1)} %get-tuple-element.23.gating_ref, bf16[128,256]{1,0:T(8,128)(2,1)S(1)} %get-tuple-element.24.mixer_ref, ...), custom_call_target="tpu_custom_call" | custom-call | tf_op jit(solution)/shard_map/finish/pallas_call | solution.py:466
  (4 shorter events, 0.0 us)
Async XLA Ops:
  44.8 17.3 %copy-start.5 = (f32[128]{0:T(128)S(1)}, f32[128]{0:T(128)}, u32[]{:S(2)}) copy-start(f32[128]{0:T(128)} %param.18) | copy-start | bytes 1540
  44.8 17.3 %copy-start.6 = (f32[128]{0:T(128)S(1)}, f32[128]{0:T(128)}, u32[]{:S(2)}) copy-start(f32[128]{0:T(128)} %param.17) | copy-start | bytes 1540
  44.8 17.3 %copy-start.1 = (f32[128]{0:T(128)S(1)}, f32[128]{0:T(128)}, u32[]{:S(2)}) copy-start(f32[128]{0:T(128)} %param.13) | copy-start | bytes 1540
  44.8 17.3 %copy-start.2 = (f32[128]{0:T(128)S(1)}, f32[128]{0:T(128)}, u32[]{:S(2)}) copy-start(f32[128]{0:T(128)} %param.14) | copy-start | bytes 1540
  44.8 17.3 %copy-start.3 = (bf16[128,64]{0,1:T(8,128)(2,1)S(1)}, bf16[128,64]{0,1:T(8,128)(2,1)}, u32[]{:S(2)}) copy-start(bf16[128,64]{0,1:T(8,128)(2,1)} %param.16) | copy-start | bytes 49156
  44.8 17.3 %copy-start.4 = (bf16[128,64]{0,1:T(8,128)(2,1)S(1)}, bf16[128,64]{0,1:T(8,128)(2,1)}, u32[]{:S(2)}) copy-start(bf16[128,64]{0,1:T(8,128)(2,1)} %param.19) | copy-start | bytes 49156
  47.8 54.6 %all-to-all-start = ((bf16[128,2,1664]{2,1,0:T(2,128)(2,1)}), bf16[128,2,1664]{2,1,0:T(2,128)(2,1)S(1)}, u32[]{:S(2)}, u32[]{:S(2)}) async-start(bf16[128,2,1664]{2,1,0:T(2,128)(2,1)} %project.1), calls=%async_computation | async-start | bytes 1703936 | tf_op jit(solution)/shard_map/all_to_all | solution.py:423
  62.2 1.1 copy-start

commit v8 on v7

--- a/solution.py
+++ b/solution.py
@@ -56,11 +56,11 @@
 
 def columns_of(rows, channels):
     parts = jnp.concatenate([*split_parts(rows), jnp.zeros_like(rows)], axis=0).astype(BF16)
-    return columns_of_parts(parts, channels)
-
-
-def columns_of_parts(parts, channels):
     both = (one_hot_rows(channels, 0, F32) + one_hot_rows(channels, 1, F32)).astype(BF16)
+    return columns_of_parts(parts, both)
+
+
+def columns_of_parts(parts, both):
     columns = nt(both, parts)
     return columns[:, 0:2] + columns[:, 2:4] + columns[:, 4:6]
 
@@ -77,6 +77,7 @@
     rep_ref,
     mask_ref,
     affine_ref,
+    hots_ref,
     weight_ref,
     history_ref,
     sems,
@@ -98,6 +99,8 @@
     ]
     for copy in copies:
         copy.start()
+    for parity in range(2):
+        hots_ref[parity] = one_hot_rows(channels, parity)
     for copy in copies[:2]:
         copy.wait()
     for at in range(which):
@@ -118,7 +121,7 @@
 
 
 def project_kernel(
-    half_ref, packed_ref, rep_ref, mask_ref, affine_ref, out_hbm, near, far, proj, inverse_ref, out_ref, sems
+    half_ref, packed_ref, rep_ref, mask_ref, affine_ref, hots_ref, out_hbm, near, far, proj, inverse_ref, out_ref, sems
 ):
     held, cols, channels = rep_ref.shape
     deep = held // 2
@@ -146,8 +149,8 @@
     mask_far = jnp.concatenate([pltpu.roll(mask_near, shift, 1)] * 2, axis=0)
     mask_near = jnp.concatenate([mask_near] * 2, axis=0)
     outs = channels // 2
-    inverse_ref[...] = format_limit / columns_of_parts(history_parts(packed_ref, outs), channels)
-    even, odd = one_hot_rows(channels, 0), one_hot_rows(channels, 1)
+    even, odd = hots_ref[0], hots_ref[1]
+    inverse_ref[...] = format_limit / columns_of_parts(history_parts(packed_ref, outs), even + odd)
     weight = jnp.concatenate(
         [
             jnp.concatenate([packed_ref[0, at * outs : (at + 1) * outs], packed_ref[1, at * outs : (at + 1) * outs]], axis=0)
@@ -204,6 +207,7 @@
 
 
 def gate_kernel(
+    half_ref,
     mine_ref,
     rep_ref,
     packed_ref,
@@ -217,6 +221,7 @@
     order_ref,
     columns_ref,
     scale_ref,
+    chosen_ref,
     near,
 ):
     rows, cols, channels = rep_ref.shape
@@ -236,6 +241,9 @@
             block = rep_ref[start : start + deep].reshape(span, channels).astype(F32)
             near[0:span, part * channels : (part + 1) * channels] = normed_rows(block, gain, bias)
         gating_ref[half] = jax.nn.sigmoid(nt(wide_gate, near[...]))
+    row = lax.broadcasted_iota(jnp.int32, chosen_ref.shape, 0)
+    col = lax.broadcasted_iota(jnp.int32, chosen_ref.shape, 1)
+    chosen_ref[...] = jnp.where(row == 2 * (col + half_ref[0] * outs), 1.0, 0.0).astype(BF16)
     columns_ref[...] = columns_of(affine_ref[...], channels)
     parts = history_parts(packed_ref, outs).astype(F32)
     lane = lax.broadcasted_iota(jnp.int32, parts.shape, 1)
@@ -318,7 +326,7 @@
 
 
 def finish_kernel(
-    half_ref, both_ref, gating_ref, mixer_ref, columns_ref, update_ref, amax_ref, mixed, *, deep, cols
+    both_ref, gating_ref, mixer_ref, columns_ref, chosen_ref, update_ref, amax_ref, mixed, *, deep, cols
 ):
     rows, wide = both_ref.shape[1:]
     channels = rows // 2
@@ -347,10 +355,7 @@
                 place = half * 2 * deep + part * deep + at
                 update_ref[place] = mixed[part * outs : (part + 1) * outs, at * cols : (at + 1) * cols]
     last = both_ref[0, :, wide - LANES :]
-    row = lax.broadcasted_iota(jnp.int32, (rows, outs), 0)
-    col = lax.broadcasted_iota(jnp.int32, (rows, outs), 1)
-    chosen = jnp.where(row == 2 * (col + half_ref[0] * outs), 1.0, 0.0).astype(BF16)
-    sums = lax.dot_general(last, chosen, (((0,), (0,)), ((), ())), preferred_element_type=F32)
+    sums = lax.dot_general(last, chosen_ref[...], (((0,), (0,)), ((), ())), preferred_element_type=F32)
     goal = span % LANES
     amax_ref[0:1, :] = sums[goal : goal + 1] + sums[goal + 1 : goal + 2] + sums[goal + 2 : goal + 3]
     amax_ref[1:2, :] = sums[goal + 3 : goal + 4] + sums[goal + 4 : goal + 5] + sums[goal + 5 : goal + 6]
@@ -385,7 +390,7 @@
     rep = pair_rep[0]
     gain, bias = in_gain[None, :], in_bias[None, :]
 
-    packed, held, mask, affine = pl.pallas_call(
+    packed, held, mask, affine, hots = pl.pallas_call(
         fetch_kernel,
         name="fetch",
         out_shape=(
@@ -393,9 +398,10 @@
             jax.ShapeDtypeStruct((rows // 2, cols, channels), BF16),
             jax.ShapeDtypeStruct((rows, cols), jnp.int32),
             jax.ShapeDtypeStruct((2, channels), F32),
+            jax.ShapeDtypeStruct((2, 2 * channels, channels), BF16),
         ),
         in_specs=[SMEM] + [HBM] * 6,
-        out_specs=(VMEM,) * 4,
+        out_specs=(VMEM,) * 5,
         scratch_shapes=[
             pltpu.VMEM((4, channels // 2, channels), BF16),
             pltpu.VMEM((2, channels // 2), F32),
@@ -408,7 +414,7 @@
         project_kernel,
         name="project",
         out_shape=pltpu.HBM((channels, 2, 2 * wide - LANES), BF16),
-        in_specs=[SMEM] + [VMEM] * 4,
+        in_specs=[SMEM] + [VMEM] * 5,
         out_specs=HBM,
         scratch_shapes=[
             pltpu.VMEM((wide, 2 * channels), BF16),
@@ -419,10 +425,10 @@
             pltpu.SemaphoreType.DMA((channels // 8,)),
         ],
         compiler_params=GRANT,
-    )(half, packed, held, mask, affine)
+    )(half, packed, held, mask, affine, hots)
     received = lax.all_to_all(message, chips, split_axis=0, concat_axis=0, tiled=True)
     mine = lax.axis_index(chips).reshape(1).astype(jnp.int32)
-    gating, mixer, order, columns, scale = pl.pallas_call(
+    gating, mixer, order, columns, scale, chosen = pl.pallas_call(
         gate_kernel,
         name="gate",
         out_shape=(
@@ -431,13 +437,14 @@
             jax.ShapeDtypeStruct((ranks * rows, groups * LANES), BF16),
             jax.ShapeDtypeStruct((2 * channels, 2), F32),
             jax.ShapeDtypeStruct((8, LANES), F32),
+            jax.ShapeDtypeStruct((2 * channels, channels // 2), BF16),
         ),
-        in_specs=[SMEM] + [VMEM] * 7,
-        out_specs=(VMEM,) * 5,
+        in_specs=[SMEM] * 2 + [VMEM] * 7,
+        out_specs=(VMEM,) * 6,
         scratch_shapes=[pltpu.VMEM((wide, 2 * channels), BF16)],
         compiler_params=GRANT,
         cost_estimate=pl.CostEstimate(flops=20_000_000_000, bytes_accessed=3_000_000, transcendentals=0),
-    )(mine, rep, packed, gate_weight.T, out_weight.T, gain, bias, jnp.stack([out_gain, out_bias]))
+    )(half, mine, rep, packed, gate_weight.T, out_weight.T, gain, bias, jnp.stack([out_gain, out_bias]))
     count = ranks * rows // 2
     left, right = pl.pallas_call(
         functools.partial(unpack_kernel, groups=groups, deep=deep, cols=cols),
@@ -470,11 +477,11 @@
             jax.ShapeDtypeStruct((rows, channels // 2, cols), BF16),
             jax.ShapeDtypeStruct((2, channels // 2), F32),
         ),
-        in_specs=[SMEM] + [VMEM] * 4,
+        in_specs=[VMEM] * 5,
         out_specs=(VMEM,) * 2,
         scratch_shapes=[pltpu.VMEM((channels, wide), BF16)],
         compiler_params=GRANT,
-    )(half, both, gating, mixer, columns)
+    )(both, gating, mixer, columns, chosen)
     return (jnp.transpose(update, (0, 2, 1))[None], new_amax)
 
 

time: 157 us -> 157 us (level)
  no operation moved by 1% of the time
where the time goes in v8:
time: 157 us
  blocking collectives  93.5 us (60%)
  waiting for transfers between devices  37.3 us (24%)
  starting transfers between devices  14.3 us (9%)
  Pallas kernels  9.63 us (6%)
    all_gather x1, blocking collectives, on_device(): packed = lax.all_gather(packed, 'col')  43 us
    all_to_all x1, blocking collectives, on_device(): lax.all_to_all(products, chips, split_axis=0, concat_axis=0, tiled=True)  38.8 us
    all_to_all x1, waiting for transfers between devices, on_device(): lax.all_to_all(message, chips, split_axis=0, concat_axis=0, tiled=True)  37.3 us
    all_to_all x1, starting transfers between devices, on_device(): lax.all_to_all(message, chips, split_axis=0, concat_axis=0, tiled=True)  14.3 us
    all_gather x1, blocking collectives, on_device(): both = lax.all_gather(right, 'col')  6.07 us
    all_gather x1, blocking collectives, on_device(): both = lax.all_gather(returned.reshape(2 * channels, -1), 'col')  5.63 us
  transfers between devices with their start and end apart: 1, of which 1 were waited for; matrix products, arithmetic and copies ran while one was open for 0% of the time, Pallas kernels for 1%

profile of v8, /device:TPU:65, one launch (start us, length us, event | category | flops | bytes accessed | tf_op | source)
XLA Modules:
  0.0 156.9 jit_solution(9627631553891760996)
XLA Ops:
  0.6 1.1 fetch.1
  1.8 43.0 %all-gather = bf16[544,128]{1,0:T(8,128)(2,1)S(1)} all-gather(bf16[272,128]{1,0:T(8,128)(2,1)S(1)} %get-tuple-element.17), channel_id=2, replica_groups=mesh['ga'=2,'gx'=16,'gy'=8,'col'=2] {'col'}, dimensions={0}, use_global_device_ids=true | all-gather | bytes 208896 | tf_op jit(solution)/shard_map/all_gather | solution.py:412
  44.8 0.0 copy-start.5
  44.8 0.0 copy-start.6
  44.8 0.0 copy-start.4
  44.8 2.9 %project.1 = bf16[128,2,1664]{2,1,0:T(2,128)(2,1)} custom-call(s32[1]{0:T(128)} %bitcast.half_ref, bf16[2,272,128]{2,1,0:T(8,128)(2,1)S(1)} %bitcast.19, bf16[20,80,128]{2,1,0:T(8,128)(2,1)S(1)} %get-tuple-element.19.rep_ref, s32[40,80]{1,0:T(8,128)S(1)} %get-tuple-element.20.mask_ref, f32[2,128]{1,0:T(2,128)S(1)} %get-tuple-element.21.affine_ref, ...), custom_call_target="tpu_custom_call" | custom-call | tf_op jit(solution)/shard_map/project/pallas_call | solution.py:413
  47.8 14.3 %all-to-all-start = ((bf16[128,2,1664]{2,1,0:T(2,128)(2,1)}), bf16[128,2,1664]{2,1,0:T(2,128)(2,1)S(1)}, u32[]{:S(2)}, u32[]{:S(2)}) async-start(bf16[128,2,1664]{2,1,0:T(2,128)(2,1)} %project.1), calls=%async_computation | async-start | bytes 1703936 | tf_op jit(solution)/shard_map/all_to_all | solution.py:429
  62.1 0.0 copy-done.5
  62.1 0.0 copy-done.6
  62.1 0.0 copy-done.1
  62.1 0.0 copy-done.2
  62.1 0.0 copy-done.3
  62.1 0.0 copy-done.4
  62.2 0.0 copy-start
  62.2 1.1 copy-done
  63.3 1.8 %gate.1 = (f32[2,128,896]{2,1,0:T(8,128)S(1)}, bf16[128,256]{1,0:T(8,128)(2,1)S(1)}, bf16[640,1024]{1,0:T(8,128)(2,1)S(1)}, f32[256,2]{1,0:T(8,128)S(1)}, f32[8,...) custom-call(s32[1]{0:T(128)} %bitcast.half_ref, s32[1]{0:T(128)} %bitcast.1.mine_ref, bf16[40,80,128]{2,1,0:T(8,128)(2,1)S(1)} %bitcast.18, ...), custom_call_target="tpu_custom_call" | custom-call | flops 20000000000 | bytes 3000000 | tf_op jit(solution)/shard_map/gate/pallas_call | solution.py:431
  65.1 37.3 %all-to-all-done.received_ref = bf16[128,2,1664]{2,1,0:T(2,128)(2,1)S(1)} async-done(((bf16[128,2,1664]{2,1,0:T(2,128)(2,1)}), bf16[128,2,1664]{2,1,0:T(2,128)(2,1)S(1)}, u32[]{:S(2)}, u32[]{:S(2)}) %all-to-all-start) | async-done | bytes 852000 | tf_op jit(solution)/shard_map/all_to_all | solution.py:429
  102.4 0.6 unpack.1
  103.0 6.1 %all-gather.1 = bf16[672,640]{1,0:T(8,128)(2,1)S(1)} all-gather(bf16[336,640]{1,0:T(8,128)(2,1)S(1)} %get-tuple-element.24), channel_id=3, replica_groups=mesh['ga'=2,'gx'=16,'gy'=8,'col'=2] {'col'}, dimensions={0}, use_global_device_ids=true | all-gather | bytes 1290240 | tf_op jit(solution)/shard_map/all_gather | solution.py:461
  109.1 1.2 triangle.1
  110.3 38.8 %all_to_all.10 = bf16[128,2,896]{2,1,0:T(2,128)(2,1)S(1)} all-to-all(bf16[128,2,896]{2,1,0:T(2,128)(2,1)S(1)} %triangle.1), channel_id=1, replica_groups=mesh['ga'=2,'gx'=16,'gy'=8,'col'=2] {'gy','gx'}, dimensions={0} | all-to-all | bytes 917504 | tf_op jit(solution)/shard_map/all_to_all | solution.py:471
  149.1 0.2 all_gather_reshape.3
  149.3 5.6 %all_gather.19.both_ref = bf16[2,256,896]{2,1,0:T(8,128)(2,1)S(1)} all-gather(bf16[1,256,896]{2,1,0:T(8,128)(2,1)S(1)} %all_gather_reshape.3), channel_id=1, replica_groups=mesh['ga'=2,'gx'=16,'gy'=8,'col'=2] {'col'}, dimensions={0}, use_global_device_ids=true | all-gather | bytes 1376256 | tf_op jit(solution)/shard_map/all_gather | solution.py:472
  154.9 2.0 %finish.1 = (bf16[40,64,80]{2,1,0:T(8,128)(2,1)}, f32[2,64]{1,0:T(2,128)}) custom-call(bf16[2,256,896]{2,1,0:T(8,128)(2,1)S(1)} %all_gather.19.both_ref, f32[2,128,896]{2,1,0:T(8,128)S(1)} %get-tuple-element.26.gating_ref, bf16[128,256]{1,0:T(8,128)(2,1)S(1)} %get-tuple-element.27.mixer_ref, f32[256,2]{1,0:T(8,128)S(1)} %get-tuple-element.28.columns_ref, ...), custom_call_target="tpu_custom_call" | custom-call | tf_op jit(solution)/shard_map/finish/pallas_call | solution.py:473
  (4 shorter events, 0.0 us)
Async XLA Ops:
  44.8 17.3 %copy-start.5 = (f32[128]{0:T(128)S(1)}, f32[128]{0:T(128)}, u32[]{:S(2)}) copy-start(f32[128]{0:T(128)} %param.18) | copy-start | bytes 1540
  44.8 17.3 %copy-start.6 = (f32[128]{0:T(128)S(1)}, f32[128]{0:T(128)}, u32[]{:S(2)}) copy-start(f32[128]{0:T(128)} %param.17) | copy-start | bytes 1540
  44.8 17.3 %copy-start.1 = (f32[128]{0:T(128)S(1)}, f32[128]{0:T(128)}, u32[]{:S(2)}) copy-start(f32[128]{0:T(128)} %param.13) | copy-start | bytes 1540
  44.8 17.3 %copy-start.2 = (f32[128]{0:T(128)S(1)}, f32[128]{0:T(128)}, u32[]{:S(2)}) copy-start(f32[128]{0:T(128)} %param.14) | copy-start | bytes 1540
  44.8 17.3 %copy-start.3 = (bf16[128,64]{0,1:T(8,128)(2,1)S(1)}, bf16[128,64]{0,1:T(8,128)(2,1)}, u32[]{:S(2)}) copy-start(bf16[128,64]{0,1:T(8,128)(2,1)} %param.16) | copy-start | bytes 49156
  44.8 17.3 %copy-start.4 = (bf16[128,64]{0,1:T(8,128)(2,1)S(1)}, bf16[128,64]{0,1:T(8,128)(2,1)}, u32[]{:S(2)}) copy-start(bf16[128,64]{0,1:T(8,128)(2,1)} %param.19) | copy-start | bytes 49156
  47.8 54.6 %all-to-all-start = ((bf16[128,2,1664]{2,1,0:T(2,128)(2,1)}), bf16[128,2,1664]{2,1,0:T(2,128)(2,1)S(1)}, u32[]{:S(2)}, u32[]{:S(2)}) async-start(bf16[128,2,1664]{2,1,0:T(2,128)(2,1)} %project.1), calls=%async_computation | async-start | bytes 1703936 | tf_op jit(solution)/shard_map/all_to_all | solution.py:429
  62.2 1.1 copy-start
